TPU v7x, 16 devices: a 4x2x1 block of a 4x4x8 slice. The times are simulated.
16 devices in a mesh: rep: 4 (over y, z, core), dp: 4 (over x).
Axes of the slice: x: 4, y: 2, z: 1, core: 2. Of those that a mesh axis runs over, the one named last changes fastest.
The devices are a block of a 4x4x8 slice.
Arguments:
- x: bfloat16 [16, 2048, 768], P(('rep', 'dp')), parts along dimension 0
- dy: bfloat16 [16, 2048, 768], P(('rep', 'dp')), parts along dimension 0
- w_gate: bfloat16 [2, 768, 3072], replicated
- w_up: bfloat16 [2, 768, 3072], replicated
- w_down: bfloat16 [2, 3072, 768], replicated
- m_w_gate: float32 [2, 768, 3072], replicated
- m_w_up: float32 [2, 768, 3072], replicated
- m_w_down: float32 [2, 3072, 768], replicated
- v_w_gate: float32 [2, 768, 3072], replicated
- v_w_up: float32 [2, 768, 3072], replicated
- v_w_down: float32 [2, 3072, 768], replicated
Outputs:
- output 1: bfloat16 [8, 768, 3072], P('rep'), parts along dimension 0
- output 2: bfloat16 [8, 768, 3072], P('rep'), parts along dimension 0
- output 3: bfloat16 [8, 3072, 768], P('rep'), parts along dimension 0
- output 4: float32 [8, 768, 3072], P('rep'), parts along dimension 0
- output 5: float32 [8, 768, 3072], P('rep'), parts along dimension 0
- output 6: float32 [8, 3072, 768], P('rep'), parts along dimension 0
- output 7: float32 [8, 768, 3072], P('rep'), parts along dimension 0
- output 8: float32 [8, 768, 3072], P('rep'), parts along dimension 0
- output 9: float32 [8, 3072, 768], P('rep'), parts along dimension 0
There are 4 independent parts. A program takes and returns all parts, laid end to end along the dimension named above; an argument that names none is the same for every part.
All inputs are finite; a program needn't handle non-finite values.
Results may differ from a plain program's by a relative error of at most 0.022.
Values are sent between devices in bfloat16 or wider.
A program may use at most 768 MiB of HBM per device.

v0:
```python
import jax
import jax.numpy as jnp
from jax import lax
from jax.sharding import PartitionSpec as P

NAMES = ("w_gate", "w_up", "w_down")


def matmul(a, w):
    return jnp.dot(a, w, preferred_element_type=jnp.float32).astype(jnp.bfloat16)


def normed(h):
    wide = h.astype(jnp.float32)
    scale = lax.rsqrt(jnp.mean(wide**2, -1, keepdims=True) + 1e-6)
    return (wide * scale).astype(jnp.bfloat16)


def layer(h, w):
    a = normed(h)
    gate = jnp.dot(a, w["w_gate"], preferred_element_type=jnp.float32)
    up = jnp.dot(a, w["w_up"], preferred_element_type=jnp.float32)
    return h + matmul((jax.nn.silu(gate) * up).astype(jnp.bfloat16), w["w_down"])


def adamw(w, m, v, g):
    m = 0.9 * m + 0.1 * g
    v = 0.95 * v + 0.05 * g * g
    step = m * lax.rsqrt(v + 1e-8) + 0.1 * w
    return (w - 0.02 * step).astype(jnp.bfloat16), m, v


def solution(mesh):
    def step(x, dy, *arrays):
        weights, m, v = (arrays[i : i + 3] for i in (0, 3, 6))
        layers = weights[0].shape[0]
        h, kept = x[0], []
        for number in range(layers):
            kept.append(h)
            h = layer(h, {name: w[number] for name, w in zip(NAMES, weights, strict=True)})
        by_h, summed = dy[0], [None] * layers
        for number in reversed(range(layers)):
            _, back = jax.vjp(lambda w, h: layer(h, w), {name: w[number] for name, w in zip(NAMES, weights, strict=True)}, kept[number])
            by_w, by_h = back(by_h)
            summed[number] = [lax.psum(by_w[name], "dp") for name in NAMES]
        gradients = [jnp.stack([summed[number][i] for number in range(layers)]).astype(jnp.float32) for i in range(3)]
        new = [adamw(w.astype(jnp.float32), m, v, g) for w, m, v, g in zip(weights, m, v, gradients, strict=True)]
        return tuple(one[which] for which in range(3) for one in new)

    return jax.shard_map(
        step,
        mesh=mesh,
        in_specs=(P(("rep", "dp"), None, None),) * 2 + (P(None, None, None),) * 9,
        out_specs=(P("rep", None, None),) * 9,
        check_vma=False,
    )
```

profile of v0, /device:TPU:112, one launch (start us, length us, event | category | flops | bytes accessed | tf_op | source)
XLA Modules:
  0.0 905.1 jit_solution(5429437452276877594)
XLA Ops:
  7.3 3.2 copy.20
  10.5 0.7 fusion.30
  11.1 5.0 copy.21
  16.2 15.8 %convolution_convert_fusion.1 = bf16[2048,3072]{1,0:T(8,128)(2,1)} fusion(bf16[2,3072,768]{2,1,0:T(8,128)(2,1)} %param.15, bf16[1,2048,768]{2,1,0:T(8,128)(2,1)} %param.12), kind=kOutput, calls=%fused_computation.52 | convolution fusion | flops 9669967872 | bytes 20447232 | tf_op jit(solution)/shard_map/transpose(jvp())/dot_general | solution.py:10
  32.0 15.9 %fusion.56 = f32[2048,3072]{1,0:T(8,128)} fusion(bf16[2,768,3072]{2,1,0:T(8,128)(2,1)} %param.13, bf16[1,2048,768]{2,1,0:T(8,128)(2,1)S(1)} %copy-done.4, f32[2048]{0:T(1024)S(1)} %add_rsqrt_fusion), kind=kOutput, calls=%fused_computation.90 | convolution fusion | flops 9668395008 | bytes 33038336 | tf_op jit(solution)/shard_map/dot_general | solution.py:21
  47.9 27.8 %multiply_convert_fusion.1 = (bf16[2048,3072]{1,0:T(8,128)(2,1)}, f32[2048,3072]{1,0:T(8,128)}) fusion(f32[2048,3072]{1,0:T(8,128)} %fusion.56, bf16[2,768,3072]{2,1,0:T(8,128)(2,1)} %param.14, bf16[1,2048,768]{2,1,0:T(8,128)(2,1)} %param.11, f32[2048]{0:T(1024)S(1)} %add_rsqrt_fusion), kind=kOutput, calls=%fused_computation.20 | convolution fusion | flops 9706143744 | bytes 70787072 | tf_op jit(solution)/shard_map/dot_general | solution.py:22
  75.7 15.1 %fusion.34 = (f32[2048]{0:T(1024)S(1)}, bf16[2048,768]{0,1:T(8,128)(2,1)S(1)}) fusion(bf16[2048,3072]{1,0:T(8,128)(2,1)} %get-tuple-element.24, bf16[2,3072,768]{2,1,0:T(8,128)(2,1)} %param.15, bf16[1,2048,768]{1,2,0:T(8,128)(2,1)S(1)} %copy.20), kind=kOutput, calls=%fused_computation.67 | convolution fusion | flops 9671538688 | bytes 23601152 | tf_op jit(solution)/shard_map/dot_general | solution.py:10
  90.8 0.6 copy-done.8
  91.4 1.1 copy-done.6
  92.5 15.7 %fusion.43 = f32[2048,3072]{1,0:T(8,128)} fusion(bf16[2,768,3072]{2,1,0:T(8,128)(2,1)} %param.14, bf16[2048,768]{0,1:T(8,128)(2,1)S(1)} %get-tuple-element.27, f32[2048]{0:T(1024)S(1)} %fusion.102), kind=kOutput, calls=%fused_computation.77 | convolution fusion | flops 9668395008 | bytes 33038336 | tf_op jit(solution)/shard_map/jvp()/dot_general | solution.py:22
  108.1 39.6 %fusion.2 = (bf16[2048,3072]{1,0:T(8,128)(2,1)}, f32[2048,3072]{1,0:T(8,128)}) fusion(f32[2048,3072]{1,0:T(8,128)} %fusion.43, bf16[2048,3072]{1,0:T(8,128)(2,1)} %convolution_convert_fusion.1, bf16[2,768,3072]{2,1,0:T(8,128)(2,1)} %param.13, bf16[2048,768]{0,1:T(8,128)(2,1)} %copy-done.6, f32[2048]{0:T(1024)S(1)} %fusion.102), kind=kOutput, calls=%fused_computation.11 | convolution fusion | flops 9743892480 | bytes 83369984 | tf_op jit(solution)/shard_map/jvp()/dot_general | solution.py:21
  147.8 18.6 %fusion.76 = bf16[2048,768]{0,1:T(8,128)(2,1)} fusion(bf16[2,768,3072]{2,1,0:T(8,128)(2,1)} %param.14, bf16[2048,3072]{1,0:T(8,128)(2,1)} %convolution_convert_fusion.1, f32[2048,3072]{1,0:T(8,128)} %get-tuple-element.29), kind=kOutput, calls=%fused_computation.107 | convolution fusion | flops 9702998016 | bytes 45613056 | tf_op jit(solution)/shard_map/transpose(jvp())/dot_general | solution.py:22
  166.4 19.6 %fusion.68 = bf16[1,768,3072]{2,1,0:T(8,128)(2,1)} fusion(bf16[2048,3072]{1,0:T(8,128)(2,1)} %convolution_convert_fusion.1, bf16[2048,768]{0,1:T(8,128)(2,1)} %copy-done.6, f32[2048]{0:T(1024)S(1)} %fusion.102, f32[2048,3072]{1,0:T(8,128)} %get-tuple-element.29), kind=kOutput, calls=%fused_computation.100 | convolution fusion | flops 9708503040 | bytes 45621248 | tf_op jit(solution)/shard_map/transpose(jvp())/dot_general | solution.py:22
  186.1 22.3 %fusion.65 = bf16[1,3072,768]{2,1,0:T(8,128)(2,1)} fusion(f32[2048,3072]{1,0:T(8,128)} %fusion.43, bf16[1,2048,768]{2,1,0:T(8,128)(2,1)S(1)} %copy-done.5, f32[2048,3072]{1,0:T(8,128)} %get-tuple-element.29), kind=kOutput, calls=%fused_computation.97 | convolution fusion | flops 9703784448 | bytes 58195968 | tf_op jit(solution)/shard_map/transpose(jvp())/dot_general | solution.py:10
  208.4 17.5 %fusion.64 = bf16[1,768,3072]{2,1,0:T(8,128)(2,1)} fusion(bf16[2048,3072]{1,0:T(8,128)(2,1)} %get-tuple-element.28, bf16[2048,768]{0,1:T(8,128)(2,1)} %copy-done.6, f32[2048]{0:T(1024)S(1)} %fusion.102), kind=kOutput, calls=%fused_computation.96 | convolution fusion | flops 9668395008 | bytes 20455424 | tf_op jit(solution)/shard_map/transpose(jvp())/dot_general | solution.py:21
  225.9 16.4 %fusion.36 = (f32[2048]{0:T(1024)S(1)}, bf16[2048,768]{0,1:T(8,128)(2,1)}) fusion(bf16[2048,768]{0,1:T(8,128)(2,1)S(1)} %copy-done.7, bf16[2048,768]{0,1:T(8,128)(2,1)} %fusion.76, bf16[2048,3072]{1,0:T(8,128)(2,1)} %get-tuple-element.28, bf16[2,768,3072]{2,1,0:T(8,128)(2,1)} %param.13), kind=kOutput, calls=%fused_computation.69 | convolution fusion | flops 9671538688 | bytes 26746880 | tf_op jit(solution)/shard_map/transpose(jvp())/dot_general | solution.py:21
  242.3 5.8 fusion.86
  248.1 14.6 %convolution_convert_fusion = bf16[2048,3072]{1,0:T(8,128)(2,1)} fusion(bf16[2048,768]{0,1:T(8,128)(2,1)} %fusion.86, bf16[2,3072,768]{2,1,0:T(8,128)(2,1)S(1)} %bitcast.81), kind=kOutput, calls=%fused_computation.51 | convolution fusion | flops 9669967872 | bytes 20447232 | tf_op jit(solution)/shard_map/transpose(jvp())/dot_general | solution.py:10
  262.7 15.6 %fusion.66 = bf16[1,3072,768]{2,1,0:T(8,128)(2,1)} fusion(bf16[2048,3072]{1,0:T(8,128)(2,1)} %get-tuple-element.24, bf16[2048,768]{0,1:T(8,128)(2,1)} %fusion.86), kind=kOutput, calls=%fused_computation.98 | convolution fusion | flops 9666035712 | bytes 20447232 | tf_op jit(solution)/shard_map/transpose(jvp())/dot_general | solution.py:10
  278.2 18.6 %fusion.67 = bf16[1,768,3072]{2,1,0:T(8,128)(2,1)} fusion(bf16[2048,3072]{1,0:T(8,128)(2,1)} %convolution_convert_fusion, f32[2048,3072]{1,0:T(8,128)} %fusion.56, bf16[1,2048,768]{1,2,0:T(8,128)(2,1)S(1)} %copy-done.1, f32[2048]{0:T(1024)S(1)} %copy-done.11), kind=kOutput, calls=%fused_computation.99 | convolution fusion | flops 9708503040 | bytes 45621248 | tf_op jit(solution)/shard_map/transpose(jvp())/dot_general | solution.py:22
  296.8 25.8 %fusion.61 = bf16[1,768,3072]{2,1,0:T(8,128)(2,1)} fusion(f32[2048,3072]{1,0:T(8,128)} %fusion.56, f32[2048,3072]{1,0:T(8,128)} %get-tuple-element.25, bf16[2048,3072]{1,0:T(8,128)(2,1)} %convolution_convert_fusion, bf16[1,2048,768]{1,2,0:T(8,128)(2,1)S(1)} %copy-done.1, f32[2048]{0:T(1024)S(1)} %copy-done.11), kind=kOutput, calls=%fused_computation.95 | convolution fusion | flops 9739960320 | bytes 70787072 | tf_op jit(solution)/shard_map/transpose(jvp())/dot_general | solution.py:21
  322.6 475.6 %all-reduce.3.cloned.1.call-done = (bf16[1,768,3072]{2,1,0:T(8,128)(2,1)}, bf16[1,768,3072]{2,1,0:T(8,128)(2,1)}, bf16[1,768,3072]{2,1,0:T(8,128)(2,1)}, bf16[1,...) async-done(((bf16[1,768,3072]{2,1,0:T(8,128)(2,1)}, bf16[1,768,3072]{2,1,0:T(8,128)(2,1)}, bf16[1,768,3072]{2,1,0:T(8,128)(2,1)}, ...) | async-done | bytes 28311568 | tf_op jit(solution)/shard_map/psum | solution.py:45
  798.2 36.7 %fusion.21 = (bf16[2,3072,768]{2,1,0:T(8,128)(2,1)}, f32[2,3072,768]{2,1,0:T(8,128)}, f32[2,3072,768]{2,1,0:T(8,128)}) fusion(bf16[2,3072,768]{2,1,0:T(8,128)(2,1)} %param.15, bf16[1,3072,768]{2,1,0:T(8,128)(2,1)} %get-tuple-element.13, bf16[1,3072,768]{2,1,0:T(8,128)(2,1)} %get-tuple-element.14, f32[2,3072,768]{2,1,0:T(8,128)} %param.21, ...), kind=kLoop, calls=%fused_computation.42 | loop fusion | flops 89653248 | bytes 103809024 | tf_op jit(solution)/shard_map/convert_element_type | solution.py:30
  834.9 63.1 %fusion.13 = (bf16[2,768,3072]{2,1,0:T(8,128)(2,1)}, f32[2,768,3072]{2,1,0:T(8,128)}, f32[2,768,3072]{2,1,0:T(8,128)}, bf16[2,768,3072]{2,1,0:T(8,128)(2,1)}, f3...) fusion(bf16[2,768,3072]{2,1,0:T(8,128)(2,1)} %param.13, bf16[1,768,3072]{2,1,0:T(8,128)(2,1)S(1)} %copy-done.3, ...), kind=kLoop, calls=%fused_computation.34 | loop fusion | flops 179306496 | bytes 207618048 | tf_op jit(solution)/shard_map/convert_element_type | solution.py:30
  (34 shorter events, 0.2 us)
Async XLA Ops:
  7.2 791.0 %all-reduce.3.cloned.1.call-start = ((), (), s32[]{:S(2)}) async-start(), calls=%async_computation | async-start | bytes 56623104 | tf_op jit(solution)/shard_map/psum | solution.py:45
  10.5 65.3 %copy-start = (bf16[1,2048,768]{1,2,0:T(8,128)(2,1)}, bf16[1,2048,768]{1,2,0:T(8,128)(2,1)S(1)}, u32[]{:S(2)}) copy-start(bf16[1,2048,768]{1,2,0:T(8,128)(2,1)S(1)} %copy.20) | copy-start | bytes 9437188
  11.1 36.8 %copy-start.10 = (f32[2048]{0:T(1024)}, f32[2048]{0:T(1024)S(1)}, u32[]{:S(2)}) copy-start(f32[2048]{0:T(1024)S(1)} %add_rsqrt_fusion) | copy-start | bytes 24580
  16.2 15.8 %copy-start.4 = (bf16[1,2048,768]{2,1,0:T(8,128)(2,1)S(1)}, bf16[1,2048,768]{2,1,0:T(8,128)(2,1)}, u32[]{:S(2)}) copy-start(bf16[1,2048,768]{2,1,0:T(8,128)(2,1)} %param.11) | copy-start | bytes 9437188
  90.8 0.6 copy-start.8
  90.8 1.7 copy-start.6
  166.4 19.7 %copy-start.5 = (bf16[1,2048,768]{2,1,0:T(8,128)(2,1)S(1)}, bf16[1,2048,768]{2,1,0:T(8,128)(2,1)}, u32[]{:S(2)}) copy-start(bf16[1,2048,768]{2,1,0:T(8,128)(2,1)} %param.12) | copy-start | bytes 9437188
  208.4 17.5 %copy-start.7 = (bf16[2048,768]{0,1:T(8,128)(2,1)S(1)}, bf16[2048,768]{0,1:T(8,128)(2,1)}, u32[]{:S(2)}) copy-start(bf16[2048,768]{0,1:T(8,128)(2,1)} %copy-done.6) | copy-start | bytes 9437188
  208.4 39.7 %slice-start = ((s8[9437184]{0:T(1024)(128)(4,1)}), s8[4194304]{0:T(1024)(128)(4,1)S(1)}, s32[]{:S(2)}) async-start(s8[9437184]{0:T(1024)(128)(4,1)} %bitcast.80), calls=%async_computation.1 | async-start | bytes 8388608
  208.4 39.7 %slice-start.1 = ((s8[9437184]{0:T(1024)(128)(4,1)}), s8[4194304]{0:T(1024)(128)(4,1)S(1)}, s32[]{:S(2)}) async-start(s8[9437184]{0:T(1024)(128)(4,1)} %bitcast.80), calls=%async_computation.2 | async-start | bytes 8388608
  225.8 16.4 %copy-start.9 = (f32[2048]{0:T(1024)S(1)}, f32[2048]{0:T(1024)}, u32[]{:S(2)}) copy-start(f32[2048]{0:T(1024)} %copy-done.8) | copy-start | bytes 24580
  225.9 16.4 %copy-start.2 = (bf16[1,2048,768]{1,2,0:T(8,128)(2,1)S(1)}, bf16[1,2048,768]{1,2,0:T(8,128)(2,1)}, u32[]{:S(2)}) copy-start(bf16[1,2048,768]{1,2,0:T(8,128)(2,1)} %copy.21) | copy-start | bytes 9437188
  225.9 22.2 %slice-start.2 = ((s8[9437184]{0:T(1024)(128)(4,1)}), s8[1048576]{0:T(1024)(128)(4,1)S(1)}, s32[]{:S(2)}) async-start(s8[9437184]{0:T(1024)(128)(4,1)} %bitcast.80), calls=%async_computation.3 | async-start | bytes 2097152
  262.7 15.6 %copy-start.1 = (bf16[1,2048,768]{1,2,0:T(8,128)(2,1)S(1)}, bf16[1,2048,768]{1,2,0:T(8,128)(2,1)}, u32[]{:S(2)}) copy-start(bf16[1,2048,768]{1,2,0:T(8,128)(2,1)} %copy-done) | copy-start | bytes 9437188
  262.7 15.6 %copy-start.11 = (f32[2048]{0:T(1024)S(1)}, f32[2048]{0:T(1024)}, u32[]{:S(2)}) copy-start(f32[2048]{0:T(1024)} %copy-done.10) | copy-start | bytes 24580
  798.2 36.7 %copy-start.3 = (bf16[1,768,3072]{2,1,0:T(8,128)(2,1)S(1)}, bf16[1,768,3072]{2,1,0:T(8,128)(2,1)}, u32[]{:S(2)}) copy-start(bf16[1,768,3072]{2,1,0:T(8,128)(2,1)} %get-tuple-element.9) | copy-start | bytes 14155780
Sparse Core Ops, SparseCore 0:
  322.8 475.3 all-reduce.2
where the time goes:
time: 913 us; the launch traced here: 905 us
  waiting for transfers between devices  476 us (52%)
  matrix products  299 us (33%)
  other arithmetic  106 us (12%)
  between operations  14.5 us (2%)
  local copies, waits for them, and re-layouts  9.93 us (1%)
    psum x1, waiting for transfers between devices, step(): summed[number] = [lax.psum(by_w[name], 'dp') for name in NAMES]  476 us
    dot_general x5, matrix products, layer(): gate = jnp.dot(a, w['w_gate'], preferred_element_type=jnp.float32)  115 us
    dot_general x5, matrix products, layer(): up = jnp.dot(a, w['w_up'], preferred_element_type=jnp.float32)  100 us
    convert_element_type x2, other arithmetic, adamw(): return ((w - 0.02 * step).astype(jnp.bfloat16), m, v)  99.7 us
    dot_general x5, matrix products, matmul(): jnp.dot(a, w, preferred_element_type=jnp.float32).astype(jnp.bfloat16)  83.4 us
  transfers between devices with their start and end apart: 1, of which 1 were waited for; matrix products, arithmetic and copies ran while one was open for 0% of the time, Pallas kernels for 0%

commit v1 on v0

v1 whole, which is shorter than its diff:
```python
import functools

import jax
import jax.numpy as jnp
from jax import lax
from jax.experimental import pallas as pl
from jax.experimental.pallas import tpu as pltpu
from jax.sharding import PartitionSpec as P


BF16, F32 = jnp.bfloat16, jnp.float32
TOKEN_BLOCK = 512
HIDDEN_BLOCK = 512
PIECE = 256
GROUP = 2
VMEM = 67043328


def nn(a, b):
    return lax.dot_general(a, b, (((1,), (0,)), ((), ())), preferred_element_type=F32)


def nt(a, b):
    return lax.dot_general(a, b, (((1,), (1,)), ((), ())), preferred_element_type=F32)


def scale_of(wide):
    return lax.rsqrt(jnp.mean(wide * wide, -1, keepdims=True) + 1e-6)


def call(kernel, after, ins, in_specs, out_specs, out_shape, *, grid, half=None, scratch=(), aliases=None, cost=0):
    after = [] if after is None else [after]
    scalars = [] if half is None else [half]
    first, last = len(scalars) + len(ins), len(scalars) + len(ins) + len(after)

    def body(*refs):
        kernel(*refs[len(scalars) : first], *refs[last:])

    return pl.pallas_call(
        body,
        grid_spec=pltpu.PrefetchScalarGridSpec(
            num_scalar_prefetch=len(scalars),
            grid=grid,
            in_specs=[*in_specs, *[pl.BlockSpec(memory_space=pl.ANY)] * len(after)],
            out_specs=out_specs,
            scratch_shapes=scratch,
        ),
        out_shape=out_shape,
        input_output_aliases=aliases or {},
        compiler_params=pltpu.CompilerParams(vmem_limit_bytes=VMEM, dimension_semantics=("arbitrary",)),
        cost_estimate=pl.CostEstimate(flops=1, bytes_accessed=cost, transcendentals=0),
    )(*scalars, *ins, *after)


def shape(*dims, dtype=BF16):
    return jax.ShapeDtypeStruct(dims, dtype)


def weight_specs(layer, d, hidden):
    once = pl.Buffered(1)
    return [
        pl.BlockSpec((None, d, hidden), lambda i: (layer, 0, 0), pipeline_mode=once),
        pl.BlockSpec((None, d, hidden), lambda i: (layer, 0, 0), pipeline_mode=once),
        pl.BlockSpec((None, hidden, d), lambda i: (layer, 0, 0), pipeline_mode=once),
    ]


def normed(h_ref, a_ref, at_ref):
    wide = h_ref[...].astype(F32)
    a = wide * scale_of(wide)
    a_ref[...] = a.astype(BF16)
    at_ref[...] = a.T.astype(BF16)


def forward_kernel(h_ref, wg_ref, wu_ref, wd_ref, a_ref, at_ref, out_ref):
    normed(h_ref, a_ref, at_ref)
    a = a_ref[...]
    hidden = wg_ref.shape[1]
    bf = min(HIDDEN_BLOCK, hidden)
    acc = None
    for j in range(hidden // bf):
        cols = pl.ds(j * bf, bf)
        g = nn(a, wg_ref[:, cols])
        u = nn(a, wu_ref[:, cols])
        act = (g * jax.nn.sigmoid(g) * u).astype(BF16)
        part = nn(act, wd_ref[cols, :])
        acc = part if acc is None else acc + part
    out_ref[...] = (h_ref[...].astype(F32) + acc.astype(BF16).astype(F32)).astype(BF16)


def forward(h, weights, layer, after):
    t, d = h.shape
    tm = min(TOKEN_BLOCK, t)
    row = pl.BlockSpec((tm, d), lambda i: (i, 0))
    col = pl.BlockSpec((d, tm), lambda i: (0, i))
    return call(
        forward_kernel,
        after,
        (h, *weights),
        [row, *weight_specs(layer, d, weights[0].shape[2])],
        [row, col, row],
        [shape(t, d), shape(d, t), shape(t, d)],
        grid=(t // tm,),
    )


def norm(h, after):
    t, d = h.shape
    tm = min(TOKEN_BLOCK, t)
    row = pl.BlockSpec((tm, d), lambda i: (i, 0))
    col = pl.BlockSpec((d, tm), lambda i: (0, i))
    return call(normed, after, (h,), [row], [row, col], [shape(t, d), shape(d, t)], grid=(t // tm,))


def turn_kernel(x_ref, xt_ref):
    xt_ref[...] = x_ref[...].T


def turn(x, after):
    t, d = x.shape
    tm = min(TOKEN_BLOCK, t)
    row = pl.BlockSpec((tm, d), lambda i: (i, 0))
    col = pl.BlockSpec((d, tm), lambda i: (0, i))
    return call(turn_kernel, after, (x,), [row], col, shape(d, t), grid=(t // tm,))


def gates(g, u, dact):
    s = jax.nn.sigmoid(g)
    silu = g * s
    act = (silu * u).astype(BF16)
    dact = dact.astype(BF16).astype(F32)
    dg = (dact * u * (s + silu * (1.0 - s))).astype(BF16)
    du = (dact * silu).astype(BF16)
    return act, dg, du


def data_kernel(h_ref, a_ref, dy_ref, wg_ref, wu_ref, wd_ref, dh_ref, dht_ref):
    a, dy = a_ref[...], dy_ref[...]
    hidden = wg_ref.shape[1]
    bf = min(HIDDEN_BLOCK, hidden)

    def three(j):
        cols = pl.ds(j * bf, bf)
        return nn(a, wg_ref[:, cols]), nn(a, wu_ref[:, cols]), nt(dy, wd_ref[cols, :])

    acc, now = None, three(0)
    for j in range(hidden // bf):
        cols = pl.ds(j * bf, bf)
        _, dg, du = gates(*now)
        if (j + 1) * bf < hidden:
            now = three(j + 1)
        part = nt(dg, wg_ref[:, cols]) + nt(du, wu_ref[:, cols])
        acc = part if acc is None else acc + part
    da = acc.astype(BF16).astype(F32)
    wide = h_ref[...].astype(F32)
    scale = scale_of(wide)
    inner = jnp.mean(da * wide, -1, keepdims=True)
    back = (scale * da - wide * (scale * scale * scale * inner)).astype(BF16)
    dh = dy.astype(F32) + back.astype(F32)
    dh_ref[...] = dh.astype(BF16)
    dht_ref[...] = dh.T.astype(BF16)


def data_gradient(h, a, dy, weights, layer, after):
    t, d = h.shape
    tm = min(TOKEN_BLOCK, t)
    row = pl.BlockSpec((tm, d), lambda i: (i, 0))
    col = pl.BlockSpec((d, tm), lambda i: (0, i))
    return call(
        data_kernel,
        after,
        (h, a, dy, *weights),
        [row, row, row, *weight_specs(layer, d, weights[0].shape[2])],
        [row, col],
        [shape(t, d), shape(d, t)],
        grid=(t // tm,),
    )


def weight_kernel(*refs):
    own, other, (wg_ref, wu_ref, wd_ref), outs, acc_ref = refs[:4], refs[4:8], refs[8:11], refs[11:-1], refs[-1]
    step = pl.program_id(0)

    @pl.when(step == 0)
    def _():
        acc_ref[...] = jnp.zeros_like(acc_ref)

    wg, wu, wd = wg_ref[...], wu_ref[...], wd_ref[...]
    for a_ref, at_ref, dy_ref, dyt_ref in (own, other):
        a, dy = a_ref[...], dy_ref[...]
        act, dg, du = gates(nn(a, wg), nn(a, wu), nt(dy, wd))
        at, dyt = at_ref[...], dyt_ref[...]
        acc_ref[0] += nn(at, dg)
        acc_ref[1] += nn(at, du)
        acc_ref[2] += nn(dyt, act)

    @pl.when(step == pl.num_programs(0) - 1)
    def _():
        for k, out_ref in enumerate(outs):
            out_ref[...] = acc_ref[:, :, k * PIECE : (k + 1) * PIECE].astype(BF16)


def weight_gradient(half, own, other, weights, layer, start, count, after):
    t, d = own[0].shape
    total = weights[0].shape[2] // (2 * PIECE)
    tm = min(TOKEN_BLOCK, t)
    row = pl.BlockSpec((tm, d), lambda i, half: (i, 0))
    col = pl.BlockSpec((d, tm), lambda i, half: (0, i))
    width = count * PIECE
    at = lambda half: (half[0] * total + start) // count
    across = pl.BlockSpec((None, d, width), lambda i, half: (layer, 0, at(half)))
    down = pl.BlockSpec((None, width, d), lambda i, half: (layer, at(half), 0))
    return call(
        weight_kernel,
        after,
        (*own, *other, *weights),
        [row, col, row, col] * 2 + [across, across, down],
        [pl.BlockSpec((3, d, PIECE), lambda i, half: (0, 0, 0))] * count,
        [shape(3, d, PIECE)] * count,
        grid=(t // tm,),
        half=half,
        scratch=[pltpu.VMEM((3, d, width), F32)],
    )


def merge_kernel(part_ref, came_ref, out_ref):
    out_ref[...] = (part_ref[...].astype(F32) + came_ref[...].astype(F32)).astype(BF16)


def merge(part, came, after):
    spec = pl.BlockSpec((1, *part.shape[1:]), lambda i: (i, 0, 0))
    return call(merge_kernel, after, (part, came), [spec] * 2, spec, shape(*part.shape), grid=(part.shape[0],))


def adamw_kernel(count, *refs):
    gs, ins, outs, token_ref = refs[:count], refs[count : count + 9], refs[-10:-1], refs[-1]
    token_ref[...] = jnp.zeros_like(token_ref)
    for k in range(3):
        g = jnp.concatenate([g_ref[k].astype(F32) for g_ref in gs], 1)
        if k == 2:
            g = g.T
        w = ins[k][...].astype(F32)
        m = 0.9 * ins[3 + k][...] + 0.1 * g
        v = 0.95 * ins[6 + k][...] + 0.05 * g * g
        step = m * lax.rsqrt(v + 1e-8) + 0.1 * w
        outs[k][...] = (w - 0.02 * step).astype(BF16)
        outs[3 + k][...] = m
        outs[6 + k][...] = v


def adamw(half, gs, arrays, so_far, layer, start, after):
    _, d, _ = gs[0].shape
    count = len(gs)
    total = arrays[0].shape[2] // (2 * PIECE)
    rows = min(256, d)
    width = count * PIECE
    at = lambda half: (half[0] * total + start) // count
    across = pl.BlockSpec((None, rows, width), lambda i, half: (layer, i, at(half)))
    down = pl.BlockSpec((None, width, rows), lambda i, half: (layer, at(half), i))
    nine = [across, across, down] * 3
    kept = [] if so_far is None else list(so_far)
    return call(
        functools.partial(adamw_kernel, count),
        after,
        (*gs, *arrays, *kept),
        [pl.BlockSpec((3, rows, PIECE), lambda i, half: (0, i, 0))] * count + nine + [pl.BlockSpec(memory_space=pl.ANY)] * len(kept),
        [*nine, pl.BlockSpec((8, 128), lambda i, half: (0, 0))],
        [*[shape(*one.shape, dtype=one.dtype) for one in arrays], shape(8, 128, dtype=F32)],
        grid=(d // rows,),
        half=half,
        aliases={1 + count + 9 + k: k for k in range(len(kept))},
    )


def solution(mesh):
    n = mesh.shape["dp"]
    pair_a = [(i, i + 1 - 2 * (i % 2)) for i in range(n)]
    pair_b = [(i, (i - 1 + 2 * (i % 2)) % n) for i in range(n)]

    def whole_step(x, dy, *arrays):
        weights = arrays[:3]
        layers, _, hidden = weights[0].shape
        pieces = hidden // (2 * PIECE)
        me = lax.axis_index("dp")
        mine = (((me + 1) // 2) % 2).astype(jnp.int32).reshape(1)
        theirs = 1 - mine
        x, dy = x[0], dy[0]
        last = [None]

        def run(f, *args):
            out = f(*args, last[0])
            last[0] = out[-1] if isinstance(out, (tuple, list)) else out
            return out

        def send(array, pairs):
            return lax.ppermute(array, "dp", pairs)

        x_other = send(x, pair_a)
        dy_other = send(dy, pair_a)

        state = {"new": None}
        sums, own_steps, other_steps = [], [], []

        def merge_next():
            layer, piece, part, came = sums.pop(0)
            whole = run(merge, part, came)
            own_steps.append((layer, piece, whole))
            other_steps.append((layer, piece, send(whole, pair_a)))

        def step_next(half, queue, most):
            taken = [queue.pop(0) for _ in range(min(most, len(queue)))]
            layer, start = taken[0][:2]
            state["new"] = run(adamw, half, [one[2] for one in taken], arrays, state["new"], layer, start)[:-1]

        def forward_all(h):
            kept = []
            for layer in range(layers - 1):
                a, at, out = run(forward, h, weights, layer)
                kept.append((h, a, at))
                h = out
            return [*kept, (h, *run(norm, h))]

        def data(side, layer):
            h, a, _ = kept[side][layer]
            return run(data_gradient, h, a, by_h[side][0], weights, layer)

        kept = [forward_all(x), None]
        by_h = [(dy, run(turn, dy)), None]
        next_own = data(0, layers - 1)
        kept[1] = forward_all(x_other)
        by_h[1] = (dy_other, run(turn, dy_other))
        for layer in reversed(range(layers)):
            sides = [(*kept[s][layer][1:], *by_h[s]) for s in range(2)]
            for start in range(0, pieces, GROUP):
                parts = run(weight_gradient, mine, *sides, weights, layer, start, GROUP)
                sums += [(layer, start + k, part, send(part, pair_b)) for k, part in enumerate(parts)]
                if len(sums) > 2:
                    merge_next()
            if layer:
                by_h = [data(0, layer) if layer < layers - 1 else next_own, data(1, layer)]
                merge_next()
                merge_next()
        while sums:
            merge_next()
            for _ in range(2):
                if len(own_steps) >= GROUP:
                    step_next(mine, own_steps, GROUP)
                elif len(other_steps) > GROUP:
                    step_next(theirs, other_steps, GROUP)
        while own_steps:
            step_next(mine, own_steps, GROUP)
        while len(other_steps) > GROUP:
            step_next(theirs, other_steps, GROUP)
        while other_steps:
            step_next(theirs, other_steps, 1)
        return tuple(state["new"])

    return jax.shard_map(
        whole_step,
        mesh=mesh,
        in_specs=(P(("rep", "dp"), None, None),) * 2 + (P(None, None, None),) * 9,
        out_specs=(P("rep", None, None),) * 9,
        check_vma=False,
    )
```

time: 913 us -> 685 us (0.75)
  Pallas kernels: 0 us -> 575 us
  waiting for transfers between devices: 476 us -> 67.9 us
  matrix products: 299 us -> 0 us
  other arithmetic: 106 us -> 0 us
  starting transfers between devices: 0.06 us -> 33.9 us
  between operations: 14.5 us -> 1.01 us
  local copies, waits for them, and re-layouts: 9.93 us -> 0 us
    pallas_call x0 -> x39, Pallas kernels: none -> 575 us  [call(): pl.pallas_call(body, grid_spec=pltpu.PrefetchScalarGridSpec(num_scalar_pr...]
    psum x1 -> x0, waiting for transfers between devices: 476 us -> none  [step(): summed[number] = [lax.psum(by_w[name], 'dp') for name in NAMES]]
    dot_general x15 -> x0, matrix products: 299 us -> none  [the longest x5 115 us: layer(): gate = jnp.dot(a, w['w_gate'], preferred_element_type=jnp.float32)]
    convert_element_type x2 -> x0, other arithmetic: 99.7 us -> none  [adamw(): return ((w - 0.02 * step).astype(jnp.bfloat16), m, v)]
    ppermute x0 -> x26, waiting for transfers between devices: none -> 67.9 us  [send(): return lax.ppermute(array, 'dp', pairs)]
    ppermute x0 -> x26, starting transfers between devices: none -> 33.9 us  [send(): return lax.ppermute(array, 'dp', pairs)]
    unnamed x32 -> x0, local copies, waits for them, and re-layouts: 9.93 us -> none
  transfers between devices with their start and end apart: 1 -> 26, of which waited for: 1 -> 6; matrix products, arithmetic and copies ran while one was open for 0% -> 0% of each run, Pallas kernels for 0% -> 79%
where the time goes in v1:
time: 685 us; the launch traced here: 678 us
  Pallas kernels  575 us (84%)
  waiting for transfers between devices  67.9 us (10%)
  starting transfers between devices  33.9 us (5%)
    pallas_call x39, Pallas kernels, call(): pl.pallas_call(body, grid_spec=pltpu.PrefetchScalarGridSpec(num_scalar_pr...  575 us
    ppermute x26, waiting for transfers between devices, send(): return lax.ppermute(array, 'dp', pairs)  67.9 us
    ppermute x26, starting transfers between devices, send(): return lax.ppermute(array, 'dp', pairs)  33.9 us
  transfers between devices with their start and end apart: 26, of which 6 were waited for; matrix products, arithmetic and copies ran while one was open for 0% of the time, Pallas kernels for 79%

profile of v1, /device:TPU:112, one launch (start us, length us, event | category | flops | bytes accessed | tf_op | source)
XLA Modules:
  0.0 678.0 jit_solution(13189512870186677944)
XLA Ops:
  3.2 38.8 %shard_map.178 = (bf16[2048,768]{1,0:T(8,128)(2,1)}, bf16[768,2048]{1,0:T(8,128)(2,1)}, bf16[2048,768]{1,0:T(8,128)(2,1)}) custom-call(bf16[2048,768]{1,0:T(8,128)(2,1)} %bitcast.10, bf16[2,768,3072]{2,1,0:T(8,128)(2,1)} %refs_2_.7, bf16[2,768,3072]{2,1,0:T(8,128)(2,1)} %refs_3_.33, bf16[2,3072,768]{2,1,0:T(8,128)(2,1)} %refs_4_.29), custom_call_target="tpu_custom_call" | custom-call | flops 1 | tf_op jit(solution)/shard_map/pallas_call | solution.py:39
  52.0 61.5 %shard_map.181 = (bf16[2048,768]{1,0:T(8,128)(2,1)}, bf16[768,2048]{1,0:T(8,128)(2,1)}) custom-call(bf16[2048,768]{1,0:T(8,128)(2,1)} %get-tuple-element.166.refs_0_.refs_1_, bf16[2048,768]{1,0:T(8,128)(2,1)} %get-tuple-element.167.refs_1_, bf16[2048,768]{1,0:T(8,128)(2,1)} %bitcast.5, bf16[2,768,3072]{2,1,0:T(8,128)(2,1)} %refs_2_.7, ...), custom_call_target="tpu_custom_call" | custom-call | flops 1 | tf_op jit(solution)/shard_map/pallas_call | solution.py:39
  113.5 38.9 %shard_map.182 = (bf16[2048,768]{1,0:T(8,128)(2,1)}, bf16[768,2048]{1,0:T(8,128)(2,1)}, bf16[2048,768]{1,0:T(8,128)(2,1)}) custom-call(bf16[2048,768]{1,0:T(8,128)(2,1)} %collective-permute-done.refs_0_, bf16[2,768,3072]{2,1,0:T(8,128)(2,1)} %refs_2_.7, bf16[2,768,3072]{2,1,0:T(8,128)(2,1)} %refs_3_.33, bf16[2,3072,768]{2,1,0:T(8,128)(2,1)} %refs_4_.29, ...), custom_call_target="tpu_custom_call" | custom-call | flops 1 | tf_op jit(solution)/shard_map/pallas_call | solution.py:39
  162.7 29.0 %shard_map.185 = (bf16[3,768,256]{2,1,0:T(8,128)(2,1)}, bf16[3,768,256]{2,1,0:T(8,128)(2,1)}) custom-call(s32[1]{0:T(128)} %bitcast.refs_0_, bf16[2048,768]{1,0:T(8,128)(2,1)} %get-tuple-element.167.refs_1_, bf16[768,2048]{1,0:T(8,128)(2,1)} %get-tuple-element.168.refs_1_.refs_2_, bf16[2048,768]{1,0:T(8,128)(2,1)} %bitcast.6, ...), custom_call_target="tpu_custom_call" | custom-call | flops 1 | tf_op jit(solution)/shard_map/pallas_call | solution.py:39
  195.3 28.9 %shard_map.186 = (bf16[3,768,256]{2,1,0:T(8,128)(2,1)}, bf16[3,768,256]{2,1,0:T(8,128)(2,1)}) custom-call(s32[1]{0:T(128)} %bitcast.refs_0_, bf16[2048,768]{1,0:T(8,128)(2,1)} %get-tuple-element.167.refs_1_, bf16[768,2048]{1,0:T(8,128)(2,1)} %get-tuple-element.168.refs_1_.refs_2_, bf16[2048,768]{1,0:T(8,128)(2,1)} %bitcast.7, ...), custom_call_target="tpu_custom_call" | custom-call | flops 1 | tf_op jit(solution)/shard_map/pallas_call | solution.py:39
  230.9 29.3 %shard_map.188 = (bf16[3,768,256]{2,1,0:T(8,128)(2,1)}, bf16[3,768,256]{2,1,0:T(8,128)(2,1)}) custom-call(s32[1]{0:T(128)} %bitcast.refs_0_, bf16[2048,768]{1,0:T(8,128)(2,1)} %get-tuple-element.167.refs_1_, bf16[768,2048]{1,0:T(8,128)(2,1)} %get-tuple-element.168.refs_1_.refs_2_, bf16[2048,768]{1,0:T(8,128)(2,1)} %bitcast.8, ...), custom_call_target="tpu_custom_call" | custom-call | flops 1 | tf_op jit(solution)/shard_map/pallas_call | solution.py:39
  267.0 61.0 %shard_map.190 = (bf16[2048,768]{1,0:T(8,128)(2,1)}, bf16[768,2048]{1,0:T(8,128)(2,1)}) custom-call(bf16[2048,768]{1,0:T(8,128)(2,1)} %get-tuple-element.173.refs_0_.refs_1_, bf16[2048,768]{1,0:T(8,128)(2,1)} %get-tuple-element.174.refs_5_.refs_1_, bf16[2048,768]{1,0:T(8,128)(2,1)} %collective-permute-done.1.refs_0_.refs_7_.refs_2_, ...), custom_call_target="tpu_custom_call" | custom-call | flops 1 | tf_op jit(solution)/shard_map/pallas_call | solution.py:39
  335.0 28.9 %shard_map.193 = (bf16[3,768,256]{2,1,0:T(8,128)(2,1)}, bf16[3,768,256]{2,1,0:T(8,128)(2,1)}) custom-call(s32[1]{0:T(128)} %bitcast.refs_0_, bf16[2048,768]{1,0:T(8,128)(2,1)} %get-tuple-element.164.refs_1_, bf16[768,2048]{1,0:T(8,128)(2,1)} %get-tuple-element.165.refs_2_, bf16[2048,768]{1,0:T(8,128)(2,1)} %get-tuple-element.169.refs_3_, ...), custom_call_target="tpu_custom_call" | custom-call | flops 1 | tf_op jit(solution)/shard_map/pallas_call | solution.py:39
  369.3 25.0 %collective-permute-done.17.refs_1_ = bf16[3,768,256]{2,1,0:T(8,128)(2,1)} collective-permute-done((bf16[3,768,256]{2,1,0:T(8,128)(2,1)}, bf16[3,768,256]{2,1,0:T(8,128)(2,1)}, u32[]{:S(2)}, u32[]{:S(2)}) %collective-permute-start.17) | collective-permute-done | bytes 1179680 | tf_op jit(solution)/shard_map/ppermute | solution.py:296
  397.8 28.9 %shard_map.195 = (bf16[3,768,256]{2,1,0:T(8,128)(2,1)}, bf16[3,768,256]{2,1,0:T(8,128)(2,1)}) custom-call(s32[1]{0:T(128)} %bitcast.refs_0_, bf16[2048,768]{1,0:T(8,128)(2,1)} %get-tuple-element.164.refs_1_, bf16[768,2048]{1,0:T(8,128)(2,1)} %get-tuple-element.165.refs_2_, bf16[2048,768]{1,0:T(8,128)(2,1)} %get-tuple-element.169.refs_3_, ...), custom_call_target="tpu_custom_call" | custom-call | flops 1 | tf_op jit(solution)/shard_map/pallas_call | solution.py:39
  433.5 28.9 %shard_map.197 = (bf16[3,768,256]{2,1,0:T(8,128)(2,1)}, bf16[3,768,256]{2,1,0:T(8,128)(2,1)}) custom-call(s32[1]{0:T(128)} %bitcast.refs_0_, bf16[2048,768]{1,0:T(8,128)(2,1)} %get-tuple-element.164.refs_1_, bf16[768,2048]{1,0:T(8,128)(2,1)} %get-tuple-element.165.refs_2_, bf16[2048,768]{1,0:T(8,128)(2,1)} %get-tuple-element.169.refs_3_, ...), custom_call_target="tpu_custom_call" | custom-call | flops 1 | tf_op jit(solution)/shard_map/pallas_call | solution.py:39
  483.7 11.3 %shard_map.200 = (bf16[2,768,3072]{2,1,0:T(8,128)(2,1)}, bf16[2,768,3072]{2,1,0:T(8,128)(2,1)}, bf16[2,3072,768]{2,1,0:T(8,128)(2,1)}, f32[2,768,3072]{2,1,0:T(8...) custom-call(s32[1]{0:T(128)} %bitcast.refs_0_, ...), custom_call_target="tpu_custom_call" | custom-call | flops 1 | tf_op jit(solution)/shard_map/pallas_call | solution.py:39
  495.0 11.4 %shard_map.201 = (bf16[2,768,3072]{2,1,0:T(8,128)(2,1)}, bf16[2,768,3072]{2,1,0:T(8,128)(2,1)}, bf16[2,3072,768]{2,1,0:T(8,128)(2,1)}, f32[2,768,3072]{2,1,0:T(8...) custom-call(s32[1]{0:T(128)} %bitcast.refs_0_, ...), custom_call_target="tpu_custom_call", output_to_operand_aliasing={{0}: (12, {}), {1}: (13, {}), {2}: (14, {}), {3}: (15, {}),... | custom-call | flops 1 | tf_op jit(solution)/shard_map/pallas_call | solution.py:39
  509.9 11.7 %shard_map.203 = (bf16[2,768,3072]{2,1,0:T(8,128)(2,1)}, bf16[2,768,3072]{2,1,0:T(8,128)(2,1)}, bf16[2,3072,768]{2,1,0:T(8,128)(2,1)}, f32[2,768,3072]{2,1,0:T(8...) custom-call(s32[1]{0:T(128)} %bitcast.refs_0_, ...), custom_call_target="tpu_custom_call", output_to_operand_aliasing={{0}: (12, {}), {1}: (13, {}), {2}: (14, {}), {3}: (15, {}),... | custom-call | flops 1 | tf_op jit(solution)/shard_map/pallas_call | solution.py:39
  521.5 11.4 %shard_map.204 = (bf16[2,768,3072]{2,1,0:T(8,128)(2,1)}, bf16[2,768,3072]{2,1,0:T(8,128)(2,1)}, bf16[2,3072,768]{2,1,0:T(8,128)(2,1)}, f32[2,768,3072]{2,1,0:T(8...) custom-call(s32[1]{0:T(128)} %bitcast.refs_0_, ...), custom_call_target="tpu_custom_call", output_to_operand_aliasing={{0}: (12, {}), {1}: (13, {}), {2}: (14, {}), {3}: (15, {}),... | custom-call | flops 1 | tf_op jit(solution)/shard_map/pallas_call | solution.py:39
  536.4 11.3 %shard_map.206 = (bf16[2,768,3072]{2,1,0:T(8,128)(2,1)}, bf16[2,768,3072]{2,1,0:T(8,128)(2,1)}, bf16[2,3072,768]{2,1,0:T(8,128)(2,1)}, f32[2,768,3072]{2,1,0:T(8...) custom-call(s32[1]{0:T(128)} %bitcast.refs_0_, ...), custom_call_target="tpu_custom_call", output_to_operand_aliasing={{0}: (12, {}), {1}: (13, {}), {2}: (14, {}), {3}: (15, {}),... | custom-call | flops 1 | tf_op jit(solution)/shard_map/pallas_call | solution.py:39
  548.4 11.3 %shard_map.207 = (bf16[2,768,3072]{2,1,0:T(8,128)(2,1)}, bf16[2,768,3072]{2,1,0:T(8,128)(2,1)}, bf16[2,3072,768]{2,1,0:T(8,128)(2,1)}, f32[2,768,3072]{2,1,0:T(8...) custom-call(s32[1]{0:T(128)S(6)} %sub.8.refs_0_, ...), custom_call_target="tpu_custom_call", output_to_operand_aliasing={{0}: (12, {}), {1}: (13, {}), {2}: (14, {}), {3}: (15, {}),... | custom-call | flops 1 | tf_op jit(solution)/shard_map/pallas_call | solution.py:39
  565.2 11.3 %shard_map.209 = (bf16[2,768,3072]{2,1,0:T(8,128)(2,1)}, bf16[2,768,3072]{2,1,0:T(8,128)(2,1)}, bf16[2,3072,768]{2,1,0:T(8,128)(2,1)}, f32[2,768,3072]{2,1,0:T(8...) custom-call(s32[1]{0:T(128)S(6)} %sub.8.refs_0_, ...), custom_call_target="tpu_custom_call", output_to_operand_aliasing={{0}: (12, {}), {1}: (13, {}), {2}: (14, {}), {3}: (15, {}),... | custom-call | flops 1 | tf_op jit(solution)/shard_map/pallas_call | solution.py:39
  578.0 11.4 %shard_map.210 = (bf16[2,768,3072]{2,1,0:T(8,128)(2,1)}, bf16[2,768,3072]{2,1,0:T(8,128)(2,1)}, bf16[2,3072,768]{2,1,0:T(8,128)(2,1)}, f32[2,768,3072]{2,1,0:T(8...) custom-call(s32[1]{0:T(128)S(6)} %sub.8.refs_0_, ...), custom_call_target="tpu_custom_call", output_to_operand_aliasing={{0}: (12, {}), {1}: (13, {}), {2}: (14, {}), {3}: (15, {}),... | custom-call | flops 1 | tf_op jit(solution)/shard_map/pallas_call | solution.py:39
  593.6 11.3 %shard_map.212 = (bf16[2,768,3072]{2,1,0:T(8,128)(2,1)}, bf16[2,768,3072]{2,1,0:T(8,128)(2,1)}, bf16[2,3072,768]{2,1,0:T(8,128)(2,1)}, f32[2,768,3072]{2,1,0:T(8...) custom-call(s32[1]{0:T(128)} %bitcast.refs_0_, ...), custom_call_target="tpu_custom_call", output_to_operand_aliasing={{0}: (12, {}), {1}: (13, {}), {2}: (14, {}), {3}: (15, {}),... | custom-call | flops 1 | tf_op jit(solution)/shard_map/pallas_call | solution.py:39
  604.9 11.4 %shard_map.213 = (bf16[2,768,3072]{2,1,0:T(8,128)(2,1)}, bf16[2,768,3072]{2,1,0:T(8,128)(2,1)}, bf16[2,3072,768]{2,1,0:T(8,128)(2,1)}, f32[2,768,3072]{2,1,0:T(8...) custom-call(s32[1]{0:T(128)S(6)} %sub.8.refs_0_, ...), custom_call_target="tpu_custom_call", output_to_operand_aliasing={{0}: (12, {}), {1}: (13, {}), {2}: (14, {}), {3}: (15, {}),... | custom-call | flops 1 | tf_op jit(solution)/shard_map/pallas_call | solution.py:39
  616.3 11.2 %collective-permute-done.22.refs_1_ = bf16[3,768,256]{2,1,0:T(8,128)(2,1)} collective-permute-done((bf16[3,768,256]{2,1,0:T(8,128)(2,1)}, bf16[3,768,256]{2,1,0:T(8,128)(2,1)}, u32[]{:S(2)}, u32[]{:S(2)}) %collective-permute-start.22) | collective-permute-done | bytes 1179680 | tf_op jit(solution)/shard_map/ppermute | solution.py:296
  627.5 11.3 %shard_map.214 = (bf16[2,768,3072]{2,1,0:T(8,128)(2,1)}, bf16[2,768,3072]{2,1,0:T(8,128)(2,1)}, bf16[2,3072,768]{2,1,0:T(8,128)(2,1)}, f32[2,768,3072]{2,1,0:T(8...) custom-call(s32[1]{0:T(128)S(6)} %sub.8.refs_0_, ...), custom_call_target="tpu_custom_call", output_to_operand_aliasing={{0}: (12, {}), {1}: (13, {}), {2}: (14, {}), {3}: (15, {}),... | custom-call | flops 1 | tf_op jit(solution)/shard_map/pallas_call | solution.py:39
  638.7 14.0 %collective-permute-done.21.refs_1_ = bf16[3,768,256]{2,1,0:T(8,128)(2,1)} collective-permute-done((bf16[3,768,256]{2,1,0:T(8,128)(2,1)}, bf16[3,768,256]{2,1,0:T(8,128)(2,1)}, u32[]{:S(2)}, u32[]{:S(2)}) %collective-permute-start.21) | collective-permute-done | bytes 1179680 | tf_op jit(solution)/shard_map/ppermute | solution.py:296
  (67 shorter events, 127.7 us)
Async XLA Ops:
  0.6 112.8 %collective-permute-start = (bf16[2048,768]{1,0:T(8,128)(2,1)}, bf16[2048,768]{1,0:T(8,128)(2,1)}, u32[]{:S(2)}, u32[]{:S(2)}) collective-permute-start(bf16[2048,768]{1,0:T(8,128)(2,1)} %bitcast.9), channel_id=1, source_target_pairs={{0,1},{1,0},{2,3},{3,2},{4,5},{5,4},{6,7},{7,6},{8,9},{9,8},{10,11... | collective-permute-start | bytes 9437192 | tf_op jit(solution)/shard_map/ppermute | solution.py:296
  3.1 154.9 %collective-permute-start.1 = (bf16[2048,768]{1,0:T(8,128)(2,1)}, bf16[2048,768]{1,0:T(8,128)(2,1)}, u32[]{:S(2)}, u32[]{:S(2)}) collective-permute-start(bf16[2048,768]{1,0:T(8,128)(2,1)} %bitcast.3), channel_id=1, source_target_pairs={{0,1},{1,0},{2,3},{3,2},{4,5},{5,4},{6,7},{7,6},{8,9},{9,8},{10,11... | collective-permute-start | bytes 9437192 | tf_op jit(solution)/shard_map/ppermute | solution.py:296
  195.2 68.2 %collective-permute-start.2 = (bf16[3,768,256]{2,1,0:T(8,128)(2,1)}, bf16[3,768,256]{2,1,0:T(8,128)(2,1)}, u32[]{:S(2)}, u32[]{:S(2)}) collective-permute-start(bf16[3,768,256]{2,1,0:T(8,128)(2,1)} %get-tuple-element.176.refs_12_.refs_0_), channel_id=1, source_target_pairs={{0,3},{1,2},{2,1},{3,0},{4,7},{5,6},{6,5},{7,4},{8,11},{9,10},{10,... | collective-permute-start | bytes 3538952 | tf_op jit(solution)/shard_map/ppermute | solution.py:296
  224.2 103.8 %collective-permute-start.7 = (bf16[3,768,256]{2,1,0:T(8,128)(2,1)}, bf16[3,768,256]{2,1,0:T(8,128)(2,1)}, u32[]{:S(2)}, u32[]{:S(2)}) collective-permute-start(bf16[3,768,256]{2,1,0:T(8,128)(2,1)} %get-tuple-element.183.refs_0_), channel_id=1, source_target_pairs={{0,3},{1,2},{2,1},{3,0},{4,7},{5,6},{6,5},{7,4},{8,11},{9,10},{10,... | collective-permute-start | bytes 3538952 | tf_op jit(solution)/shard_map/ppermute | solution.py:296
  227.3 104.2 %collective-permute-start.6 = (bf16[3,768,256]{2,1,0:T(8,128)(2,1)}, bf16[3,768,256]{2,1,0:T(8,128)(2,1)}, u32[]{:S(2)}, u32[]{:S(2)}) collective-permute-start(bf16[3,768,256]{2,1,0:T(8,128)(2,1)} %get-tuple-element.178.refs_2_.refs_0_), channel_id=1, source_target_pairs={{0,3},{1,2},{2,1},{3,0},{4,7},{5,6},{6,5},{7,4},{8,11},{9,10},{10,... | collective-permute-start | bytes 3538952 | tf_op jit(solution)/shard_map/ppermute | solution.py:296
  260.2 106.9 %collective-permute-start.5 = (bf16[3,768,256]{2,1,0:T(8,128)(2,1)}, bf16[3,768,256]{2,1,0:T(8,128)(2,1)}, u32[]{:S(2)}, u32[]{:S(2)}) collective-permute-start(bf16[3,768,256]{2,1,0:T(8,128)(2,1)} %get-tuple-element.182.refs_0_), channel_id=1, source_target_pairs={{0,3},{1,2},{2,1},{3,0},{4,7},{5,6},{6,5},{7,4},{8,11},{9,10},{10,... | collective-permute-start | bytes 3538952 | tf_op jit(solution)/shard_map/ppermute | solution.py:296
  266.9 102.3 %collective-permute-start.4 = (bf16[3,768,256]{2,1,0:T(8,128)(2,1)}, bf16[3,768,256]{2,1,0:T(8,128)(2,1)}, u32[]{:S(2)}, u32[]{:S(2)}) collective-permute-start(bf16[3,768,256]{2,1,0:T(8,128)(2,1)} %get-tuple-element.179.refs_2_.refs_0_), channel_id=1, source_target_pairs={{0,3},{1,2},{2,1},{3,0},{4,7},{5,6},{6,5},{7,4},{8,11},{9,10},{10,... | collective-permute-start | bytes 3538952 | tf_op jit(solution)/shard_map/ppermute | solution.py:296
  367.1 59.6 %collective-permute-start.16 = (bf16[3,768,256]{2,1,0:T(8,128)(2,1)}, bf16[3,768,256]{2,1,0:T(8,128)(2,1)}, u32[]{:S(2)}, u32[]{:S(2)}) collective-permute-start(bf16[3,768,256]{2,1,0:T(8,128)(2,1)} %get-tuple-element.184.refs_2_.refs_0_), channel_id=1, source_target_pairs={{0,3},{1,2},{2,1},{3,0},{4,7},{5,6},{6,5},{7,4},{8,11},{9,10},{10,... | collective-permute-start | bytes 3538952 | tf_op jit(solution)/shard_map/ppermute | solution.py:296
  367.2 62.7 %collective-permute-start.14 = (bf16[3,768,256]{2,1,0:T(8,128)(2,1)}, bf16[3,768,256]{2,1,0:T(8,128)(2,1)}, u32[]{:S(2)}, u32[]{:S(2)}) collective-permute-start(bf16[3,768,256]{2,1,0:T(8,128)(2,1)} %shard_map.189.refs_6_.refs_2_), channel_id=1, source_target_pairs={{0,1},{1,0},{2,3},{3,2},{4,5},{5,4},{6,7},{7,6},{8,9},{9,8},{10,11... | collective-permute-start | bytes 3538952 | tf_op jit(solution)/shard_map/ppermute | solution.py:296
  367.2 95.2 %collective-permute-start.13 = (bf16[3,768,256]{2,1,0:T(8,128)(2,1)}, bf16[3,768,256]{2,1,0:T(8,128)(2,1)}, u32[]{:S(2)}, u32[]{:S(2)}) collective-permute-start(bf16[3,768,256]{2,1,0:T(8,128)(2,1)} %shard_map.187.refs_12_.refs_1_), channel_id=1, source_target_pairs={{0,1},{1,0},{2,3},{3,2},{4,5},{5,4},{6,7},{7,6},{8,9},{9,8},{10,11... | collective-permute-start | bytes 3538952 | tf_op jit(solution)/shard_map/ppermute | solution.py:296
  369.2 96.4 %collective-permute-start.12 = (bf16[3,768,256]{2,1,0:T(8,128)(2,1)}, bf16[3,768,256]{2,1,0:T(8,128)(2,1)}, u32[]{:S(2)}, u32[]{:S(2)}) collective-permute-start(bf16[3,768,256]{2,1,0:T(8,128)(2,1)} %shard_map.192.refs_12_.refs_2_), channel_id=1, source_target_pairs={{0,1},{1,0},{2,3},{3,2},{4,5},{5,4},{6,7},{7,6},{8,9},{9,8},{10,11... | collective-permute-start | bytes 3538952 | tf_op jit(solution)/shard_map/ppermute | solution.py:296
  394.3 77.9 %collective-permute-start.11 = (bf16[3,768,256]{2,1,0:T(8,128)(2,1)}, bf16[3,768,256]{2,1,0:T(8,128)(2,1)}, u32[]{:S(2)}, u32[]{:S(2)}) collective-permute-start(bf16[3,768,256]{2,1,0:T(8,128)(2,1)} %shard_map.191.refs_2_.refs_1_), channel_id=1, source_target_pairs={{0,1},{1,0},{2,3},{3,2},{4,5},{5,4},{6,7},{7,6},{8,9},{9,8},{10,11... | collective-permute-start | bytes 3538952 | tf_op jit(solution)/shard_map/ppermute | solution.py:296
  426.6 45.5 %collective-permute-start.15 = (bf16[3,768,256]{2,1,0:T(8,128)(2,1)}, bf16[3,768,256]{2,1,0:T(8,128)(2,1)}, u32[]{:S(2)}, u32[]{:S(2)}) collective-permute-start(bf16[3,768,256]{2,1,0:T(8,128)(2,1)} %get-tuple-element.187.refs_0_), channel_id=1, source_target_pairs={{0,3},{1,2},{2,1},{3,0},{4,7},{5,6},{6,5},{7,4},{8,11},{9,10},{10,... | collective-permute-start | bytes 3538952 | tf_op jit(solution)/shard_map/ppermute | solution.py:296
  429.9 52.5 %collective-permute-start.18 = (bf16[3,768,256]{2,1,0:T(8,128)(2,1)}, bf16[3,768,256]{2,1,0:T(8,128)(2,1)}, u32[]{:S(2)}, u32[]{:S(2)}) collective-permute-start(bf16[3,768,256]{2,1,0:T(8,128)(2,1)} %get-tuple-element.185.refs_2_.refs_0_), channel_id=1, source_target_pairs={{0,3},{1,2},{2,1},{3,0},{4,7},{5,6},{6,5},{7,4},{8,11},{9,10},{10,... | collective-permute-start | bytes 3538952 | tf_op jit(solution)/shard_map/ppermute | solution.py:296
  462.4 85.3 %collective-permute-start.19 = (bf16[3,768,256]{2,1,0:T(8,128)(2,1)}, bf16[3,768,256]{2,1,0:T(8,128)(2,1)}, u32[]{:S(2)}, u32[]{:S(2)}) collective-permute-start(bf16[3,768,256]{2,1,0:T(8,128)(2,1)} %get-tuple-element.248.refs_0_), channel_id=1, source_target_pairs={{0,3},{1,2},{2,1},{3,0},{4,7},{5,6},{6,5},{7,4},{8,11},{9,10},{10,... | collective-permute-start | bytes 3538952 | tf_op jit(solution)/shard_map/ppermute | solution.py:296
  465.6 97.6 %collective-permute-start.10 = (bf16[3,768,256]{2,1,0:T(8,128)(2,1)}, bf16[3,768,256]{2,1,0:T(8,128)(2,1)}, u32[]{:S(2)}, u32[]{:S(2)}) collective-permute-start(bf16[3,768,256]{2,1,0:T(8,128)(2,1)} %shard_map.196.refs_12_.refs_2_), channel_id=1, source_target_pairs={{0,1},{1,0},{2,3},{3,2},{4,5},{5,4},{6,7},{7,6},{8,9},{9,8},{10,11... | collective-permute-start | bytes 3538952 | tf_op jit(solution)/shard_map/ppermute | solution.py:296
  472.2 92.4 %collective-permute-start.9 = (bf16[3,768,256]{2,1,0:T(8,128)(2,1)}, bf16[3,768,256]{2,1,0:T(8,128)(2,1)}, u32[]{:S(2)}, u32[]{:S(2)}) collective-permute-start(bf16[3,768,256]{2,1,0:T(8,128)(2,1)} %shard_map.194.refs_12_.refs_1_), channel_id=1, source_target_pairs={{0,1},{1,0},{2,3},{3,2},{4,5},{5,4},{6,7},{7,6},{8,9},{9,8},{10,11... | collective-permute-start | bytes 3538952 | tf_op jit(solution)/shard_map/ppermute | solution.py:296
  472.2 104.4 %collective-permute-start.8 = (bf16[3,768,256]{2,1,0:T(8,128)(2,1)}, bf16[3,768,256]{2,1,0:T(8,128)(2,1)}, u32[]{:S(2)}, u32[]{:S(2)}) collective-permute-start(bf16[3,768,256]{2,1,0:T(8,128)(2,1)} %get-tuple-element.186.refs_2_.refs_0_), channel_id=1, source_target_pairs={{0,3},{1,2},{2,1},{3,0},{4,7},{5,6},{6,5},{7,4},{8,11},{9,10},{10,... | collective-permute-start | bytes 3538952 | tf_op jit(solution)/shard_map/ppermute | solution.py:296
  482.4 110.6 %collective-permute-start.25 = (bf16[3,768,256]{2,1,0:T(8,128)(2,1)}, bf16[3,768,256]{2,1,0:T(8,128)(2,1)}, u32[]{:S(2)}, u32[]{:S(2)}) collective-permute-start(bf16[3,768,256]{2,1,0:T(8,128)(2,1)} %shard_map.199.refs_12_.refs_2_), channel_id=1, source_target_pairs={{0,1},{1,0},{2,3},{3,2},{4,5},{5,4},{6,7},{7,6},{8,9},{9,8},{10,11... | collective-permute-start | bytes 3538952 | tf_op jit(solution)/shard_map/ppermute | solution.py:296
  547.7 57.2 %collective-permute-start.24 = (bf16[3,768,256]{2,1,0:T(8,128)(2,1)}, bf16[3,768,256]{2,1,0:T(8,128)(2,1)}, u32[]{:S(2)}, u32[]{:S(2)}) collective-permute-start(bf16[3,768,256]{2,1,0:T(8,128)(2,1)} %shard_map.198.refs_2_.refs_1_), channel_id=1, source_target_pairs={{0,1},{1,0},{2,3},{3,2},{4,5},{5,4},{6,7},{7,6},{8,9},{9,8},{10,11... | collective-permute-start | bytes 3538952 | tf_op jit(solution)/shard_map/ppermute | solution.py:296
  563.2 53.0 %collective-permute-start.23 = (bf16[3,768,256]{2,1,0:T(8,128)(2,1)}, bf16[3,768,256]{2,1,0:T(8,128)(2,1)}, u32[]{:S(2)}, u32[]{:S(2)}) collective-permute-start(bf16[3,768,256]{2,1,0:T(8,128)(2,1)} %shard_map.205.refs_2_.refs_21_), channel_id=1, source_target_pairs={{0,1},{1,0},{2,3},{3,2},{4,5},{5,4},{6,7},{7,6},{8,9},{9,8},{10,11... | collective-permute-start | bytes 3538952 | tf_op jit(solution)/shard_map/ppermute | solution.py:296
  564.6 62.9 %collective-permute-start.22 = (bf16[3,768,256]{2,1,0:T(8,128)(2,1)}, bf16[3,768,256]{2,1,0:T(8,128)(2,1)}, u32[]{:S(2)}, u32[]{:S(2)}) collective-permute-start(bf16[3,768,256]{2,1,0:T(8,128)(2,1)} %shard_map.202.refs_21_.refs_1_), channel_id=1, source_target_pairs={{0,1},{1,0},{2,3},{3,2},{4,5},{5,4},{6,7},{7,6},{8,9},{9,8},{10,11... | collective-permute-start | bytes 3538952 | tf_op jit(solution)/shard_map/ppermute | solution.py:296
  576.5 76.2 %collective-permute-start.21 = (bf16[3,768,256]{2,1,0:T(8,128)(2,1)}, bf16[3,768,256]{2,1,0:T(8,128)(2,1)}, u32[]{:S(2)}, u32[]{:S(2)}) collective-permute-start(bf16[3,768,256]{2,1,0:T(8,128)(2,1)} %shard_map.208.refs_21_.refs_1_), channel_id=1, source_target_pairs={{0,1},{1,0},{2,3},{3,2},{4,5},{5,4},{6,7},{7,6},{8,9},{9,8},{10,11... | collective-permute-start | bytes 3538952 | tf_op jit(solution)/shard_map/ppermute | solution.py:296
  592.9 77.9 %collective-permute-start.20 = (bf16[3,768,256]{2,1,0:T(8,128)(2,1)}, bf16[3,768,256]{2,1,0:T(8,128)(2,1)}, u32[]{:S(2)}, u32[]{:S(2)}) collective-permute-start(bf16[3,768,256]{2,1,0:T(8,128)(2,1)} %shard_map.211.refs_2_.refs_21_), channel_id=1, source_target_pairs={{0,1},{1,0},{2,3},{3,2},{4,5},{5,4},{6,7},{7,6},{8,9},{9,8},{10,11... | collective-permute-start | bytes 3538952 | tf_op jit(solution)/shard_map/ppermute | solution.py:296
  (2 other events, 66.0 us)

commit v2 on v1

v2 whole, which is shorter than its diff:
```python
import functools

import jax
import jax.numpy as jnp
from jax import lax
from jax.experimental import pallas as pl
from jax.experimental.pallas import tpu as pltpu
from jax.sharding import PartitionSpec as P


BF16, F32 = jnp.bfloat16, jnp.float32
TOKEN_BLOCK = 512
HIDDEN_BLOCK = 512
PIECE = 256
GROUP = 2
VMEM = 67043328


def nn(a, b):
    return lax.dot_general(a, b, (((1,), (0,)), ((), ())), preferred_element_type=F32)


def nt(a, b):
    return lax.dot_general(a, b, (((1,), (1,)), ((), ())), preferred_element_type=F32)


def scale_of(wide):
    return lax.rsqrt(jnp.mean(wide * wide, -1, keepdims=True) + 1e-6)


def call(kernel, after, ins, in_specs, out_specs, out_shape, *, grid, half=None, with_half=False, scratch=(), aliases=None, cost=0):
    after = [] if after is None else [after]
    scalars = [] if half is None else [half]
    first, last = len(scalars) + len(ins), len(scalars) + len(ins) + len(after)

    def body(*refs):
        kernel(*refs[0 if with_half else len(scalars) : first], *refs[last:])

    return pl.pallas_call(
        body,
        grid_spec=pltpu.PrefetchScalarGridSpec(
            num_scalar_prefetch=len(scalars),
            grid=grid,
            in_specs=[*in_specs, *[pl.BlockSpec(memory_space=pl.ANY)] * len(after)],
            out_specs=out_specs,
            scratch_shapes=scratch,
        ),
        out_shape=out_shape,
        input_output_aliases=aliases or {},
        compiler_params=pltpu.CompilerParams(vmem_limit_bytes=VMEM, dimension_semantics=("arbitrary",)),
        cost_estimate=pl.CostEstimate(flops=1, bytes_accessed=cost, transcendentals=0),
    )(*scalars, *ins, *after)


def shape(*dims, dtype=BF16):
    return jax.ShapeDtypeStruct(dims, dtype)


def weight_specs(layer, d, hidden):
    once = pl.Buffered(1)
    return [
        pl.BlockSpec((None, d, hidden), lambda i: (layer, 0, 0), pipeline_mode=once),
        pl.BlockSpec((None, d, hidden), lambda i: (layer, 0, 0), pipeline_mode=once),
        pl.BlockSpec((None, hidden, d), lambda i: (layer, 0, 0), pipeline_mode=once),
    ]


def normed(h_ref, a_ref, at_ref):
    wide = h_ref[...].astype(F32)
    a = wide * scale_of(wide)
    a_ref[...] = a.astype(BF16)
    at_ref[...] = a.T.astype(BF16)


def forward_kernel(h_ref, wg_ref, wu_ref, wd_ref, a_ref, at_ref, out_ref, *next_refs):
    normed(h_ref, a_ref, at_ref)
    a = a_ref[...]
    hidden = wg_ref.shape[1]
    bf = min(HIDDEN_BLOCK, hidden)
    cols = lambda j: pl.ds(j * bf, bf)
    two = lambda j: (nn(a, wg_ref[:, cols(j)]), nn(a, wu_ref[:, cols(j)]))
    acc, now = None, two(0)
    for j in range(hidden // bf):
        g, u = now
        act = (g * jax.nn.sigmoid(g) * u).astype(BF16)
        if (j + 1) * bf < hidden:
            now = two(j + 1)
        part = nn(act, wd_ref[cols(j), :])
        acc = part if acc is None else acc + part
    out_ref[...] = (h_ref[...].astype(F32) + acc.astype(BF16).astype(F32)).astype(BF16)
    if next_refs:
        normed(out_ref, *next_refs)


def forward(h, weights, layer, also_next, after):
    t, d = h.shape
    tm = min(TOKEN_BLOCK, t)
    row = pl.BlockSpec((tm, d), lambda i: (i, 0))
    col = pl.BlockSpec((d, tm), lambda i: (0, i))
    return call(
        forward_kernel,
        after,
        (h, *weights),
        [row, *weight_specs(layer, d, weights[0].shape[2])],
        [row, col, row] + [row, col] * also_next,
        [shape(t, d), shape(d, t), shape(t, d)] + [shape(t, d), shape(d, t)] * also_next,
        grid=(t // tm,),
    )


def norm(h, after):
    t, d = h.shape
    tm = min(TOKEN_BLOCK, t)
    row = pl.BlockSpec((tm, d), lambda i: (i, 0))
    col = pl.BlockSpec((d, tm), lambda i: (0, i))
    return call(normed, after, (h,), [row], [row, col], [shape(t, d), shape(d, t)], grid=(t // tm,))


def gates(g, u, dact):
    s = jax.nn.sigmoid(g)
    silu = g * s
    act = (silu * u).astype(BF16)
    dact = dact.astype(BF16).astype(F32)
    dg = (dact * u * (s + silu * (1.0 - s))).astype(BF16)
    du = (dact * silu).astype(BF16)
    return act, dg, du


def data_kernel(saved, keep, beside, half_ref, h_ref, a_ref, dy_ref, wg_ref, wu_ref, wd_ref, *refs):
    n_beside = len(beside.ins) if beside else 0
    saved_refs, beside_ins, refs = refs[:saved], refs[saved : saved + n_beside], refs[saved + n_beside :]
    dh_ref, dht_ref, *kept_refs = refs
    if beside:
        kept_refs, beside_outs = kept_refs[:-9], kept_refs[-9:]
        beside.run(beside_ins, beside_outs)
    saved_width = sum(ref.shape[1] for ref in saved_refs[::2])
    a, dy = a_ref[...], dy_ref[...]
    hidden = wg_ref.shape[1]
    bf = min(HIDDEN_BLOCK, hidden)
    blocks = hidden // bf
    if keep:
        kept_refs[0][...] = dy.T

    def cols(j):
        return pl.ds(pl.multiple_of(lax.rem(half_ref[0] * (blocks // 2) + j, blocks) * bf, bf), bf)

    def read(refs, j):
        out, at = [], 0
        for ref in refs:
            if j * bf <= at < (j + 1) * bf:
                out.append(ref[...])
            at += ref.shape[1]
        return jnp.concatenate(out, 1)

    def three(j):
        if j * bf < saved_width:
            return None
        return nn(a, wg_ref[:, cols(j)]), nn(a, wu_ref[:, cols(j)]), nt(dy, wd_ref[cols(j), :])

    acc, now = None, three(0)
    for j in range(blocks):
        if j * bf < saved_width:
            dg, du = read(saved_refs[::2], j), read(saved_refs[1::2], j)
        else:
            act, dg, du = gates(*now)
        if j + 1 < blocks:
            now = three(j + 1)
        if keep and j < blocks // 2:
            for ref, value in zip(kept_refs[1:], (act, dg, du), strict=True):
                ref[:, pl.ds(j * bf, bf)] = value
        part = nt(dg, wg_ref[:, cols(j)]) + nt(du, wu_ref[:, cols(j)])
        acc = part if acc is None else acc + part
    da = acc.astype(BF16).astype(F32)
    wide = h_ref[...].astype(F32)
    scale = scale_of(wide)
    inner = jnp.mean(da * wide, -1, keepdims=True)
    back = (scale * da - wide * (scale * scale * scale * inner)).astype(BF16)
    dh = dy.astype(F32) + back.astype(F32)
    dh_ref[...] = dh.astype(BF16)
    dht_ref[...] = dh.T.astype(BF16)


def data_gradient(half, h, a, dy, weights, layer, saved, keep, jobs, arrays, so_far, after):
    t, d = h.shape
    hidden = weights[0].shape[2]
    tm = min(TOKEN_BLOCK, t)
    row = pl.BlockSpec((tm, d), lambda i, half: (i, 0))
    col = pl.BlockSpec((d, tm), lambda i, half: (0, i))
    once = pl.Buffered(1)
    across = pl.BlockSpec((None, d, hidden), lambda i, half: (layer, 0, 0), pipeline_mode=once)
    down = pl.BlockSpec((None, hidden, d), lambda i, half: (layer, 0, 0), pipeline_mode=once)
    wide = pl.BlockSpec((tm, hidden // 2), lambda i, half: (i, 0))
    ins = [h, a, dy, *weights, *saved]
    specs = [row, row, row, across, across, down] + [pl.BlockSpec((tm, one.shape[1]), lambda i, half: (i, 0)) for one in saved]
    out_specs = [row, col] + [col, wide, wide, wide] * keep
    out_shapes = [shape(t, d), shape(d, t)] + [shape(d, t), *[shape(t, hidden // 2)] * 3] * keep
    aliases = {}
    beside = Beside(jobs, arrays, so_far, t // tm) if jobs else None
    if beside:
        ins += beside.ins
        specs += beside.in_specs
        aliases = {1 + len(ins) - beside.n_kept + k: len(out_specs) + k for k in range(beside.n_kept)}
        out_specs = out_specs + beside.out_specs
        out_shapes = out_shapes + beside.out_shapes
    return call(
        functools.partial(data_kernel, len(saved), keep, beside),
        after,
        ins,
        specs,
        out_specs,
        out_shapes,
        grid=(t // tm,),
        half=half,
        with_half=True,
        aliases=aliases,
    )


def weight_kernel(kinds, count, keep, beside, *refs):
    refs = list(refs)
    take = lambda n: [refs.pop(0) for _ in range(n)]
    sides = [take({"kept": 5, "turned": 4, "plain": 3}[kind]) for kind in kinds]
    wg_ref, wu_ref, wd_ref = take(3)
    beside_ins = take(len(beside.ins)) if beside else None
    outs = take(count)
    beside_outs = take(9) if beside else None
    acc_ref = refs.pop()
    step = pl.program_id(0)

    @pl.when(step == 0)
    def _():
        acc_ref[...] = jnp.zeros_like(acc_ref)

    wg, wu, wd = wg_ref[...], wu_ref[...], wd_ref[...]
    raw = [None if kind == "kept" else (nn(side[0][...], wg), nn(side[0][...], wu), nt(side[2][...], wd)) for kind, side in zip(kinds, sides, strict=True)]
    terms = []
    for kind, side, dots in zip(kinds, sides, raw, strict=True):
        if kind == "kept":
            terms.append([ref[...] for ref in side])
            continue
        act, dg, du = gates(*dots)
        if kind == "turned":
            dyt = side[3][...]
        else:
            dyt = side[2][...].T
            refs.pop(0)[...] = dyt
        if keep:
            refs.pop(0)[...] = dg
            refs.pop(0)[...] = du
        terms.append([side[1][...], dyt, act, dg, du])
    at, dyt = (jnp.concatenate([term[k] for term in terms], 1) for k in range(2))
    act, dg, du = (jnp.concatenate([term[k] for term in terms], 0) for k in range(2, 5))
    acc_ref[0] += nn(at, dg)
    acc_ref[1] += nn(at, du)
    acc_ref[2] += nn(dyt, act)

    if beside:
        beside.run(beside_ins, beside_outs)

    @pl.when(step == pl.num_programs(0) - 1)
    def _():
        for k, out_ref in enumerate(outs):
            out_ref[...] = acc_ref[:, :, k * PIECE : (k + 1) * PIECE].astype(BF16)


def weight_gradient(half, sides, weights, layer, start, count, keep, jobs, arrays, so_far, after):
    d, hidden = weights[0].shape[1:]
    total = hidden // (2 * PIECE)
    t = sides[0][0].size // d
    tm = min(TOKEN_BLOCK if jobs else TOKEN_BLOCK // 2, t)
    row = pl.BlockSpec((tm, d), lambda i, half: (i, 0))
    col = pl.BlockSpec((d, tm), lambda i, half: (0, i))
    width = count * PIECE
    at = lambda half: (half[0] * total + start) // count
    across = pl.BlockSpec((None, d, width), lambda i, half: (layer, 0, at(half)))
    down = pl.BlockSpec((None, width, d), lambda i, half: (layer, at(half), 0))
    block = pl.BlockSpec((tm, width), lambda i, half: (i, start // count))
    first = pl.BlockSpec((tm, width), lambda i, half: (i, 0))
    kinds, specs, more, more_shapes = [], [], [], []
    for side in sides:
        if len(side) == 5:
            kinds.append("kept")
            specs += [col, col, block, block, block]
            continue
        kinds.append("plain" if side[3] is None else "turned")
        specs += [row, col, row] + [col] * (side[3] is not None)
        if side[3] is None:
            more.append(col)
            more_shapes.append(shape(d, t))
        more += [first, first] * keep
        more_shapes += [shape(t, width)] * 2 * keep
    ins = [one for side in sides for one in side if one is not None] + list(weights)
    specs += [across, across, down]
    out_specs, out_shapes, aliases = [pl.BlockSpec((3, d, PIECE), lambda i, half: (0, 0, 0))] * count, [shape(3, d, PIECE)] * count, {}
    beside = Beside(jobs, arrays, so_far, t // tm) if jobs else None
    if beside:
        ins += beside.ins
        specs += beside.in_specs
        aliases = {1 + len(ins) - beside.n_kept + k: count + k for k in range(beside.n_kept)}
        out_specs = out_specs + beside.out_specs
        out_shapes = out_shapes + beside.out_shapes
    return call(
        functools.partial(weight_kernel, kinds, count, keep, beside),
        after,
        ins,
        specs,
        out_specs + more,
        out_shapes + more_shapes,
        grid=(t // tm,),
        half=half,
        aliases=aliases,
        scratch=[pltpu.VMEM((3, d, width), F32)],
    )


def adamw_block(g, w_ref, m_ref, v_ref, new_w_ref, new_m_ref, new_v_ref):
    w = w_ref[...].astype(F32)
    m = 0.9 * m_ref[...] + 0.1 * g
    v = 0.95 * v_ref[...] + 0.05 * g * g
    step = m * lax.rsqrt(v + 1e-8) + 0.1 * w
    new_w_ref[...] = (w - 0.02 * step).astype(BF16)
    new_m_ref[...] = m
    new_v_ref[...] = v


def adamw_kernel(count, *refs):
    gs, ins, token_ref, outs = refs[:count], refs[count : count + 9], refs[-10], refs[-9:]
    token_ref[...] = jnp.zeros_like(token_ref)
    for k in range(3):
        g = jnp.concatenate([g_ref[k].astype(F32) for g_ref in gs], 1)
        adamw_block(g.T if k == 2 else g, *ins[k::3], *outs[k::3])


def adamw(half, gs, arrays, so_far, layer, start, after):
    _, d, _ = gs[0].shape
    count = len(gs)
    total = arrays[0].shape[2] // (2 * PIECE)
    rows = min(256, d)
    width = count * PIECE
    at = lambda half: (half[0] * total + start) // count
    across = pl.BlockSpec((None, rows, width), lambda i, half: (layer, i, at(half)))
    down = pl.BlockSpec((None, width, rows), lambda i, half: (layer, at(half), i))
    nine = [across, across, down] * 3
    kept = [] if so_far is None else list(so_far)
    return call(
        functools.partial(adamw_kernel, count),
        after,
        (*gs, *arrays, *kept),
        [pl.BlockSpec((3, rows, PIECE), lambda i, half: (0, i, 0))] * count + nine + [pl.BlockSpec(memory_space=pl.ANY)] * len(kept),
        [pl.BlockSpec((8, 128), lambda i, half: (0, 0)), *nine],
        [shape(8, 128, dtype=F32), *[shape(*one.shape, dtype=one.dtype) for one in arrays]],
        grid=(d // rows,),
        half=half,
        aliases={1 + count + 9 + k: 1 + k for k in range(len(kept))},
    )


class Beside:
    def __init__(self, jobs, arrays, so_far, steps):
        self.jobs, self.each = jobs, steps // len(jobs)
        self.count = len(jobs[0][1])
        d, hidden = arrays[0].shape[1:]
        total = hidden // (2 * PIECE)
        rows, cols = d // self.each, self.count * PIECE // self.each
        self.split = PIECE // cols
        one = lambda k, i: jnp.clip(i - k * self.each, 0, self.each - 1)

        def pick(i, values):
            out = values[0]
            for k in range(1, len(values)):
                out = jnp.where(i < k * self.each, out, values[k])
            return out

        halves = lambda half: [half[0] if own else 1 - half[0] for own, *_ in jobs]
        layer = lambda i: pick(i, [job[2] for job in jobs])
        group = lambda i, half: pick(i, [(h * total + job[3]) // self.count for h, job in zip(halves(half), jobs, strict=True)])
        across = pl.BlockSpec((None, rows, self.count * PIECE), lambda i, half: (layer(i), i % self.each, group(i, half)))
        down = pl.BlockSpec((None, cols, d), lambda i, half: (layer(i), group(i, half) * self.each + i % self.each, 0))
        nine = [across, across, down] * 3
        kept = [] if so_far is None else list(so_far)
        self.ins, self.in_specs = [], []
        for k, job in enumerate(jobs):
            for g in job[1]:
                self.ins += [g, g]
                self.in_specs.append(pl.BlockSpec((2, rows, PIECE), lambda i, half, k=k: (0, one(k, i), 0)))
                self.in_specs.append(pl.BlockSpec((1, d, cols), lambda i, half, k=k: (2, 0, one(k, i) % self.split)))
        self.ins += [*arrays, *kept]
        self.in_specs += nine + [pl.BlockSpec(memory_space=pl.ANY)] * len(kept)
        self.out_specs = nine
        self.out_shapes = [shape(*a.shape, dtype=a.dtype) for a in arrays]
        self.n_kept = len(kept)

    def run(self, ins, outs):
        step = pl.program_id(0)
        gs = [ins[2 * self.count * k : 2 * self.count * (k + 1)] for k in range(len(self.jobs))]
        nine = ins[2 * self.count * len(self.jobs) :][:9]

        def chosen(of):
            out = of(gs[0])
            for k in range(1, len(gs)):
                out = jnp.where(step < k * self.each, out, of(gs[k]))
            return out

        def third(refs):
            out = refs[1][0].astype(F32)
            for p in range(1, self.count):
                out = jnp.where(lax.rem(step, self.each) // self.split < p, out, refs[2 * p + 1][0].astype(F32))
            return out

        for k in range(2):
            g = chosen(lambda refs, k=k: jnp.concatenate([ref[k].astype(F32) for ref in refs[::2]], 1))
            adamw_block(g, *nine[k::3], *outs[k::3])
        adamw_block(chosen(third).T, *nine[2::3], *outs[2::3])


def adamw_jobs_kernel(beside, *refs):
    ins, token_ref, outs = refs[: len(beside.ins)], refs[-10], refs[-9:]
    token_ref[...] = jnp.zeros_like(token_ref)
    beside.run(ins, outs)


def adamw_jobs(half, jobs, arrays, so_far, after):
    steps = 4 * len(jobs)
    beside = Beside(jobs, arrays, so_far, steps)
    return call(
        functools.partial(adamw_jobs_kernel, beside),
        after,
        beside.ins,
        beside.in_specs,
        [pl.BlockSpec((8, 128), lambda i, half: (0, 0)), *beside.out_specs],
        [shape(8, 128, dtype=F32), *beside.out_shapes],
        grid=(steps,),
        half=half,
        aliases={1 + len(beside.ins) - beside.n_kept + k: 1 + k for k in range(beside.n_kept)},
    )


def solution(mesh):
    n = mesh.shape["dp"]
    pair_a = [(i, i + 1 - 2 * (i % 2)) for i in range(n)]
    pair_b = [(i, (i - 1 + 2 * (i % 2)) % n) for i in range(n)]

    def whole_step(x, dy, *arrays):
        weights = arrays[:3]
        layers, _, hidden = weights[0].shape
        pieces = hidden // (2 * PIECE)
        me = lax.axis_index("dp")
        mine = (((me + 1) // 2) % 2).astype(jnp.int32).reshape(1)
        theirs = 1 - mine
        x, dy = x[0], dy[0]
        last = [None]

        def run(f, *args):
            out = f(*args, last[0])
            last[0] = out[0]
            return out

        def send(array, pairs):
            return lax.ppermute(array, "dp", pairs)

        x_other = send(x, pair_a)
        dy_other = send(dy, pair_a)

        state = {"new": None}
        sums, own_steps, other_steps = [], [], []

        def merge_next():
            layer, piece, part, came = sums.pop(0)
            part, came, _ = lax.optimization_barrier((part, came, last[0]))
            whole = (part.astype(F32) + came.astype(F32)).astype(BF16)
            own_steps.append((layer, piece, whole))
            other_steps.append((layer, piece, send(whole, pair_a)))

        def step_next(half, queue, most):
            taken = [queue.pop(0) for _ in range(min(most, len(queue)))]
            layer, start = taken[0][:2]
            state["new"] = run(adamw, half, [one[2] for one in taken], arrays, state["new"], layer, start)[1:]

        def job(own, queue):
            taken = [queue.pop(0) for _ in range(GROUP)]
            return own, [one[2] for one in taken], *taken[0][:2]

        def forward_all(h):
            kept = []
            for layer in range(layers - 1):
                a, at, out, *following = run(forward, h, weights, layer, layer == layers - 2)
                kept.append((h, a, at))
                h = out
            return [*kept, (h, *(following if layers > 1 else run(norm, h)))]

        def data(side, layer, saved, keep, jobs=()):
            h, a, _ = kept[side][layer]
            out = run(data_gradient, mine, h, a, by_h[side][0], weights, layer, saved, keep, jobs, arrays, state["new"])
            if jobs:
                out, state["new"] = out[: -len(arrays)], out[-len(arrays) :]
            return out

        kept = [forward_all(x), None]
        by_h = [(dy, None), (dy_other, None)]
        next_own, next_own_t, *own_last = data(0, layers - 1, [], True)
        kept[1] = forward_all(x_other)
        for layer in reversed(range(layers)):
            is_last, keep = layer == layers - 1, layer > 0
            saved = [[], []]
            start = 0
            while start < pieces:
                group = 1 if is_last and start < GROUP else GROUP
                sides = [(*kept[s][layer][1:], *by_h[s]) for s in range(2)]
                if is_last:
                    sides[0] = (kept[0][layer][2], *own_last)
                jobs = []
                if not is_last and start == 0 and len(other_steps) >= 2 * GROUP:
                    jobs.append(job(False, other_steps))
                elif not is_last and start == GROUP and len(own_steps) >= GROUP:
                    jobs.append(job(True, own_steps))
                made = run(weight_gradient, mine, sides, weights, layer, start, group, keep, jobs, arrays, state["new"])
                sums += [(layer, start + k, part, send(part, pair_b)) for k, part in enumerate(made[:group])]
                if jobs:
                    state["new"] = made[group : group + len(arrays)]
                made = list(made[group + (len(arrays) if jobs else 0) :])
                for s in range(2):
                    if len(sides[s]) == 4:
                        if sides[s][3] is None:
                            by_h[s] = (by_h[s][0], made.pop(0))
                        if keep:
                            saved[s] += [made.pop(0), made.pop(0)]
                while len(sums) > (3 if is_last or start else 2):
                    merge_next()
                if not is_last and start == GROUP:
                    if len(own_steps) >= GROUP:
                        state["new"] = run(adamw_jobs, mine, [job(True, own_steps)], arrays, state["new"])[1:]
                    merge_next()
                start += group
            if layer:
                own = (next_own, next_own_t) if is_last else data(0, layer, saved[0], False)
                jobs = [job(True, own_steps)] if len(own_steps) >= GROUP else []
                by_h = [own, data(1, layer, saved[1], False, jobs)]
                while len(sums) > 1:
                    merge_next()

        def steps_now():
            jobs = [job(True, own_steps)] if len(own_steps) >= GROUP else []
            if len(other_steps) >= 2 * GROUP:
                jobs.append(job(False, other_steps))
            if jobs:
                state["new"] = run(adamw_jobs, mine, jobs, arrays, state["new"])[1:]
            return jobs

        steps_now()
        while sums:
            merge_next()
            steps_now()
        while steps_now():
            pass
        while other_steps:
            step_next(theirs, other_steps, 1)
        return tuple(state["new"])

    return jax.shard_map(
        whole_step,
        mesh=mesh,
        in_specs=(P(("rep", "dp"), None, None),) * 2 + (P(None, None, None),) * 9,
        out_specs=(P("rep", None, None),) * 9,
        check_vma=False,
    )
```

time: 685 us -> 619 us (0.904)
  Pallas kernels: 575 us -> 474 us
  other arithmetic: 0 us -> 34.6 us
    pallas_call x39 -> x18, Pallas kernels: 575 us -> 474 us  [call(): pl.pallas_call(body, grid_spec=pltpu.PrefetchScalarGridSpec(num_scalar_pr...]
    convert_element_type x0 -> x12, other arithmetic: none -> 34.6 us  [merge_next(): whole = (part.astype(F32) + came.astype(F32)).astype(BF16)]
  transfers between devices with their start and end apart: 26 -> 26, of which waited for: 6 -> 7; matrix products, arithmetic and copies ran while one was open for 0% -> 6% of each run, Pallas kernels for 79% -> 71%
where the time goes in v2:
time: 619 us; the launch traced here: 613 us
  Pallas kernels  474 us (77%)
  waiting for transfers between devices  69.9 us (11%)
  other arithmetic  34.6 us (6%)
  starting transfers between devices  33 us (5%)
    pallas_call x18, Pallas kernels, call(): pl.pallas_call(body, grid_spec=pltpu.PrefetchScalarGridSpec(num_scalar_pr...  474 us
    ppermute x26, waiting for transfers between devices, send(): return lax.ppermute(array, 'dp', pairs)  69.9 us
    convert_element_type x12, other arithmetic, merge_next(): whole = (part.astype(F32) + came.astype(F32)).astype(BF16)  34.6 us
    ppermute x26, starting transfers between devices, send(): return lax.ppermute(array, 'dp', pairs)  33 us
  transfers between devices with their start and end apart: 26, of which 7 were waited for; matrix products, arithmetic and copies ran while one was open for 6% of the time, Pallas kernels for 71%

profile of v2, /device:TPU:112, one launch (start us, length us, event | category | flops | bytes accessed | tf_op | source)
XLA Modules:
  0.0 612.7 jit_solution(16256558834554233004)
XLA Ops:
  3.2 39.8 %shard_map.178 = (bf16[2048,768]{1,0:T(8,128)(2,1)}, bf16[768,2048]{1,0:T(8,128)(2,1)}, bf16[2048,768]{1,0:T(8,128)(2,1)}, bf16[2048,768]{1,0:T(8,128)(2,1)}, bf16[768,2048]{1,0:T(8,128)(2,1)}) custom-call(bf16[2048,768]{1,0:T(8,128)(2,1)} %bitcast.4, bf16[2,768,3072]{2,1,0:T(8,128)(2,1)} %refs_2_.7, bf16[2,768,3072]{2,1,0:T(8,128)(2,1)} %refs_3_.7, ...), custom_call_target="tpu_custom_call" | custom-call | flops 1 | tf_op jit(solution)/shard_map/pallas_call | solution.py:39
  42.9 64.5 %shard_map.179 = (bf16[2048,768]{1,0:T(8,128)(2,1)}, bf16[768,2048]{1,0:T(8,128)(2,1)}, bf16[768,2048]{1,0:T(8,128)(2,1)}, bf16[2048,1536]{1,0:T(8,128)(2,1)}, b...) custom-call(s32[1]{0:T(128)} %bitcast.refs_0_, bf16[2048,768]{1,0:T(8,128)(2,1)} %get-tuple-element.170.refs_1_, ...), custom_call_target="tpu_custom_call" | custom-call | flops 1 | tf_op jit(solution)/shard_map/pallas_call | solution.py:39
  107.5 40.0 %shard_map.180 = (bf16[2048,768]{1,0:T(8,128)(2,1)}, bf16[768,2048]{1,0:T(8,128)(2,1)}, bf16[2048,768]{1,0:T(8,128)(2,1)}, bf16[2048,768]{1,0:T(8,128)(2,1)}, bf16[768,2048]{1,0:T(8,128)(2,1)}) custom-call(bf16[2048,768]{1,0:T(8,128)(2,1)} %collective-permute-done.refs_0_, bf16[2,768,3072]{2,1,0:T(8,128)(2,1)} %refs_2_.7, bf16[2,768,3072]{2,1,0:T(8,128)(2,1)} %refs_3_.7, ...), custom_call_target="tpu_custom_call" | custom-call | flops 1 | tf_op jit(solution)/shard_map/pallas_call | solution.py:39
  147.5 16.4 %shard_map.181 = (bf16[3,768,256]{2,1,0:T(8,128)(2,1)}, bf16[768,2048]{1,0:T(8,128)(2,1)}, bf16[2048,256]{1,0:T(8,128)(2,1)}, bf16[2048,256]{1,0:T(8,128)(2,1)}) custom-call(s32[1]{0:T(128)} %bitcast.refs_0_, bf16[768,2048]{1,0:T(8,128)(2,1)} %get-tuple-element.178.refs_1_, bf16[768,2048]{1,0:T(8,128)(2,1)} %get-tuple-element.179.refs_2_, ...), custom_call_target="tpu_custom_call" | custom-call | flops 1 | tf_op jit(solution)/shard_map/pallas_call | solution.py:39
  163.8 16.4 %shard_map.182 = (bf16[3,768,256]{2,1,0:T(8,128)(2,1)}, bf16[2048,256]{1,0:T(8,128)(2,1)}, bf16[2048,256]{1,0:T(8,128)(2,1)}) custom-call(s32[1]{0:T(128)} %bitcast.refs_0_, bf16[768,2048]{1,0:T(8,128)(2,1)} %get-tuple-element.178.refs_1_, bf16[768,2048]{1,0:T(8,128)(2,1)} %get-tuple-element.179.refs_2_, bf16[2048,1536]{1,0:T(8,128)(2,1)} %get-tuple-element.180.refs_3_, ...), custom_call_target="tpu_custom_call" | custom-call | flops 1 | tf_op jit(solution)/shard_map/pallas_call | solution.py:39
  183.8 22.7 %shard_map.183 = (bf16[3,768,256]{2,1,0:T(8,128)(2,1)}, bf16[3,768,256]{2,1,0:T(8,128)(2,1)}, bf16[2048,512]{1,0:T(8,128)(2,1)}, bf16[2048,512]{1,0:T(8,128)(2,1)}) custom-call(s32[1]{0:T(128)} %bitcast.refs_0_, bf16[768,2048]{1,0:T(8,128)(2,1)} %get-tuple-element.178.refs_1_, bf16[768,2048]{1,0:T(8,128)(2,1)} %get-tuple-element.179.refs_2_, ...), custom_call_target="tpu_custom_call" | custom-call | flops 1 | tf_op jit(solution)/shard_map/pallas_call | solution.py:39
  209.8 22.7 %shard_map.184 = (bf16[3,768,256]{2,1,0:T(8,128)(2,1)}, bf16[3,768,256]{2,1,0:T(8,128)(2,1)}, bf16[2048,512]{1,0:T(8,128)(2,1)}, bf16[2048,512]{1,0:T(8,128)(2,1)}) custom-call(s32[1]{0:T(128)} %bitcast.refs_0_, bf16[768,2048]{1,0:T(8,128)(2,1)} %get-tuple-element.178.refs_1_, bf16[768,2048]{1,0:T(8,128)(2,1)} %get-tuple-element.179.refs_2_, ...), custom_call_target="tpu_custom_call" | custom-call | flops 1 | tf_op jit(solution)/shard_map/pallas_call | solution.py:39
  244.0 55.9 %shard_map.185 = (bf16[2048,768]{1,0:T(8,128)(2,1)}, bf16[768,2048]{1,0:T(8,128)(2,1)}, bf16[2,768,3072]{2,1,0:T(8,128)(2,1)}, bf16[2,768,3072]{2,1,0:T(8,128)(2...) custom-call(s32[1]{0:T(128)} %bitcast.refs_0_, ...), custom_call_target="tpu_custom_call" | custom-call | flops 1 | tf_op jit(solution)/shard_map/pallas_call | solution.py:39
  306.2 35.0 %shard_map.186 = (bf16[3,768,256]{2,1,0:T(8,128)(2,1)}, bf16[3,768,256]{2,1,0:T(8,128)(2,1)}, bf16[2,768,3072]{2,1,0:T(8,128)(2,1)}, bf16[2,768,3072]{2,1,0:T(8,...) custom-call(s32[1]{0:T(128)} %bitcast.refs_0_, ...), custom_call_target="tpu_custom_call", output_to_operand_aliasing={{2}: (25, {}), {3}: (26, {}), {4}: (27, {}), {5}: (28, {}),... | custom-call | flops 1 | tf_op jit(solution)/shard_map/pallas_call | solution.py:39
  351.7 34.7 %shard_map.187 = (bf16[3,768,256]{2,1,0:T(8,128)(2,1)}, bf16[3,768,256]{2,1,0:T(8,128)(2,1)}, bf16[2,768,3072]{2,1,0:T(8,128)(2,1)}, bf16[2,768,3072]{2,1,0:T(8,...) custom-call(s32[1]{0:T(128)} %bitcast.refs_0_, ...), custom_call_target="tpu_custom_call", output_to_operand_aliasing={{2}: (25, {}), {3}: (26, {}), {4}: (27, {}), {5}: (28, {}),... | custom-call | flops 1 | tf_op jit(solution)/shard_map/pallas_call | solution.py:39
  392.7 10.9 %shard_map.188 = (f32[8,128]{1,0:T(8,128)}, bf16[2,768,3072]{2,1,0:T(8,128)(2,1)}, bf16[2,768,3072]{2,1,0:T(8,128)(2,1)}, bf16[2,3072,768]{2,1,0:T(8,128)(2,1)},...) custom-call(s32[1]{0:T(128)} %bitcast.refs_0_, ...), custom_call_target="tpu_custom_call", output_to_operand_aliasing={{1}: (14, {}), {2}: (15, {}), {3}: (16, {}), {4}: (17, {}),... | custom-call | flops 1 | tf_op jit(solution)/shard_map/pallas_call | solution.py:39
  403.7 28.3 %shard_map.189 = (bf16[3,768,256]{2,1,0:T(8,128)(2,1)}, bf16[3,768,256]{2,1,0:T(8,128)(2,1)}) custom-call(s32[1]{0:T(128)} %bitcast.refs_0_, bf16[2048,768]{1,0:T(8,128)(2,1)} %get-tuple-element.168.refs_7_.refs_1_, bf16[768,2048]{1,0:T(8,128)(2,1)} %get-tuple-element.169.refs_2_, bf16[2048,768]{1,0:T(8,128)(2,1)} %get-tuple-element.172.refs_4_.refs_3_, ...), custom_call_target="tpu_custom_call" | custom-call | flops 1 | tf_op jit(solution)/shard_map/pallas_call | solution.py:39
  441.3 6.2 %collective-permute-done.15 = bf16[3,768,256]{2,1,0:T(8,128)(2,1)} collective-permute-done((bf16[3,768,256]{2,1,0:T(8,128)(2,1)}, bf16[3,768,256]{2,1,0:T(8,128)(2,1)}, u32[]{:S(2)}, u32[]{:S(2)}) %collective-permute-start.15) | collective-permute-done | bytes 1179680 | tf_op jit(solution)/shard_map/ppermute | solution.py:459
  447.5 20.8 %shard_map.190 = (f32[8,128]{1,0:T(8,128)}, bf16[2,768,3072]{2,1,0:T(8,128)(2,1)}, bf16[2,768,3072]{2,1,0:T(8,128)(2,1)}, bf16[2,3072,768]{2,1,0:T(8,128)(2,1)},...) custom-call(s32[1]{0:T(128)} %bitcast.refs_0_, ...), custom_call_target="tpu_custom_call", output_to_operand_aliasing={{1}: (18, {}), {2}: (19, {}), {3}: (20, {}), {4}: (21, {}),... | custom-call | flops 1 | tf_op jit(solution)/shard_map/pallas_call | solution.py:39
  474.7 20.8 %shard_map.191 = (f32[8,128]{1,0:T(8,128)}, bf16[2,768,3072]{2,1,0:T(8,128)(2,1)}, bf16[2,768,3072]{2,1,0:T(8,128)(2,1)}, bf16[2,3072,768]{2,1,0:T(8,128)(2,1)},...) custom-call(s32[1]{0:T(128)} %bitcast.refs_0_, ...), custom_call_target="tpu_custom_call", output_to_operand_aliasing={{1}: (18, {}), {2}: (19, {}), {3}: (20, {}), {4}: (21, {}),... | custom-call | flops 1 | tf_op jit(solution)/shard_map/pallas_call | solution.py:39
  500.5 11.2 %collective-permute-done.12.refs_1_.refs_2_ = bf16[3,768,256]{2,1,0:T(8,128)(2,1)} collective-permute-done((bf16[3,768,256]{2,1,0:T(8,128)(2,1)}, bf16[3,768,256]{2,1,0:T(8,128)(2,1)}, u32[]{:S(2)}, u32[]{:S(2)}) %collective-permute-start.12) | collective-permute-done | bytes 1179680 | tf_op jit(solution)/shard_map/ppermute | solution.py:459
  511.7 11.0 %shard_map.192 = (f32[8,128]{1,0:T(8,128)}, bf16[2,768,3072]{2,1,0:T(8,128)(2,1)}, bf16[2,768,3072]{2,1,0:T(8,128)(2,1)}, bf16[2,3072,768]{2,1,0:T(8,128)(2,1)},...) custom-call(s32[1]{0:T(128)} %bitcast.refs_0_, ...), custom_call_target="tpu_custom_call", output_to_operand_aliasing={{1}: (14, {}), {2}: (15, {}), {3}: (16, {}), {4}: (17, {}),... | custom-call | flops 1 | tf_op jit(solution)/shard_map/pallas_call | solution.py:39
  526.3 10.7 %collective-permute-done.25.refs_7_.refs_8_ = bf16[3,768,256]{2,1,0:T(8,128)(2,1)} collective-permute-done((bf16[3,768,256]{2,1,0:T(8,128)(2,1)}, bf16[3,768,256]{2,1,0:T(8,128)(2,1)}, u32[]{:S(2)}, u32[]{:S(2)}) %collective-permute-start.25) | collective-permute-done | bytes 1179680 | tf_op jit(solution)/shard_map/ppermute | solution.py:459
  537.0 25.3 %collective-permute-done.24.refs_5_.refs_6_ = bf16[3,768,256]{2,1,0:T(8,128)(2,1)} collective-permute-done((bf16[3,768,256]{2,1,0:T(8,128)(2,1)}, bf16[3,768,256]{2,1,0:T(8,128)(2,1)}, u32[]{:S(2)}, u32[]{:S(2)}) %collective-permute-start.24) | collective-permute-done | bytes 1179680 | tf_op jit(solution)/shard_map/ppermute | solution.py:459
  562.3 20.8 %shard_map.193 = (f32[8,128]{1,0:T(8,128)}, bf16[2,768,3072]{2,1,0:T(8,128)(2,1)}, bf16[2,768,3072]{2,1,0:T(8,128)(2,1)}, bf16[2,3072,768]{2,1,0:T(8,128)(2,1)},...) custom-call(s32[1]{0:T(128)} %bitcast.refs_0_, ...), custom_call_target="tpu_custom_call", output_to_operand_aliasing={{1}: (18, {}), {2}: (19, {}), {3}: (20, {}), {4}: (21, {}),... | custom-call | flops 1 | tf_op jit(solution)/shard_map/pallas_call | solution.py:39
  583.1 4.5 collective-permute-done.23.refs_1_
  587.6 6.7 %shard_map.194 = (f32[8,128]{1,0:T(8,128)}, bf16[2,768,3072]{2,1,0:T(8,128)(2,1)}, bf16[2,768,3072]{2,1,0:T(8,128)(2,1)}, bf16[2,3072,768]{2,1,0:T(8,128)(2,1)},...) custom-call(s32[1]{0:T(128)S(6)} %sub.8.refs_0_, ...), custom_call_target="tpu_custom_call", output_to_operand_aliasing={{1}: (11, {}), {2}: (12, {}), {3}: (13, {}), {4}: (14, {}),... | custom-call | flops 1 | tf_op jit(solution)/shard_map/pallas_call | solution.py:39
  594.3 11.3 %collective-permute-done.21.refs_1_ = bf16[3,768,256]{2,1,0:T(8,128)(2,1)} collective-permute-done((bf16[3,768,256]{2,1,0:T(8,128)(2,1)}, bf16[3,768,256]{2,1,0:T(8,128)(2,1)}, u32[]{:S(2)}, u32[]{:S(2)}) %collective-permute-start.21) | collective-permute-done | bytes 1179680 | tf_op jit(solution)/shard_map/ppermute | solution.py:459
  605.7 6.7 %shard_map.195 = (f32[8,128]{1,0:T(8,128)}, bf16[2,768,3072]{2,1,0:T(8,128)(2,1)}, bf16[2,768,3072]{2,1,0:T(8,128)(2,1)}, bf16[2,3072,768]{2,1,0:T(8,128)(2,1)},...) custom-call(s32[1]{0:T(128)S(6)} %sub.8.refs_0_, ...), custom_call_target="tpu_custom_call", output_to_operand_aliasing={{1}: (11, {}), {2}: (12, {}), {3}: (13, {}), {4}: (14, {}),... | custom-call | flops 1 | tf_op jit(solution)/shard_map/pallas_call | solution.py:39
  (62 shorter events, 68.3 us)
Async XLA Ops:
  0.6 106.8 %collective-permute-start = (bf16[2048,768]{1,0:T(8,128)(2,1)}, bf16[2048,768]{1,0:T(8,128)(2,1)}, u32[]{:S(2)}, u32[]{:S(2)}) collective-permute-start(bf16[2048,768]{1,0:T(8,128)(2,1)} %bitcast.3), channel_id=1, source_target_pairs={{0,1},{1,0},{2,3},{3,2},{4,5},{5,4},{6,7},{7,6},{8,9},{9,8},{10,11... | collective-permute-start | bytes 9437192 | tf_op jit(solution)/shard_map/ppermute | solution.py:459
  3.1 144.4 %collective-permute-start.1 = (bf16[2048,768]{1,0:T(8,128)(2,1)}, bf16[2048,768]{1,0:T(8,128)(2,1)}, u32[]{:S(2)}, u32[]{:S(2)}) collective-permute-start(bf16[2048,768]{1,0:T(8,128)(2,1)} %bitcast.5), channel_id=1, source_target_pairs={{0,1},{1,0},{2,3},{3,2},{4,5},{5,4},{6,7},{7,6},{8,9},{9,8},{10,11... | collective-permute-start | bytes 9437192 | tf_op jit(solution)/shard_map/ppermute | solution.py:459
  180.2 52.3 %collective-permute-start.3 = (bf16[3,768,256]{2,1,0:T(8,128)(2,1)}, bf16[3,768,256]{2,1,0:T(8,128)(2,1)}, u32[]{:S(2)}, u32[]{:S(2)}) collective-permute-start(bf16[3,768,256]{2,1,0:T(8,128)(2,1)} %get-tuple-element.199.refs_13_), channel_id=1, source_target_pairs={{0,3},{1,2},{2,1},{3,0},{4,7},{5,6},{6,5},{7,4},{8,11},{9,10},{10,... | collective-permute-start | bytes 3538952 | tf_op jit(solution)/shard_map/ppermute | solution.py:459
  183.7 52.4 %collective-permute-start.2 = (bf16[3,768,256]{2,1,0:T(8,128)(2,1)}, bf16[3,768,256]{2,1,0:T(8,128)(2,1)}, u32[]{:S(2)}, u32[]{:S(2)}) collective-permute-start(bf16[3,768,256]{2,1,0:T(8,128)(2,1)} %get-tuple-element.196.refs_13_), channel_id=1, source_target_pairs={{0,3},{1,2},{2,1},{3,0},{4,7},{5,6},{6,5},{7,4},{8,11},{9,10},{10,... | collective-permute-start | bytes 3538952 | tf_op jit(solution)/shard_map/ppermute | solution.py:459
  206.6 93.3 %collective-permute-start.9 = (bf16[3,768,256]{2,1,0:T(8,128)(2,1)}, bf16[3,768,256]{2,1,0:T(8,128)(2,1)}, u32[]{:S(2)}, u32[]{:S(2)}) collective-permute-start(bf16[3,768,256]{2,1,0:T(8,128)(2,1)} %get-tuple-element.221), channel_id=1, source_target_pairs={{0,3},{1,2},{2,1},{3,0},{4,7},{5,6},{6,5},{7,4},{8,11},{9,10},{10,... | collective-permute-start | bytes 3538952 | tf_op jit(solution)/shard_map/ppermute | solution.py:459
  236.2 70.0 %collective-permute-start.7 = (bf16[3,768,256]{2,1,0:T(8,128)(2,1)}, bf16[3,768,256]{2,1,0:T(8,128)(2,1)}, u32[]{:S(2)}, u32[]{:S(2)}) collective-permute-start(bf16[3,768,256]{2,1,0:T(8,128)(2,1)} %add_convert_fusion.10.refs_17_.refs_18_), channel_id=1, source_target_pairs={{0,1},{1,0},{2,3},{3,2},{4,5},{5,4},{6,7},{7,6},{8,9},{9,8},{10,11... | collective-permute-start | bytes 3538952 | tf_op jit(solution)/shard_map/ppermute | solution.py:459
  239.2 67.0 %collective-permute-start.6 = (bf16[3,768,256]{2,1,0:T(8,128)(2,1)}, bf16[3,768,256]{2,1,0:T(8,128)(2,1)}, u32[]{:S(2)}, u32[]{:S(2)}) collective-permute-start(bf16[3,768,256]{2,1,0:T(8,128)(2,1)} %add_convert_fusion.11.refs_15_.refs_16_), channel_id=1, source_target_pairs={{0,1},{1,0},{2,3},{3,2},{4,5},{5,4},{6,7},{7,6},{8,9},{9,8},{10,11... | collective-permute-start | bytes 3538952 | tf_op jit(solution)/shard_map/ppermute | solution.py:459
  240.8 100.5 %collective-permute-start.8 = (bf16[3,768,256]{2,1,0:T(8,128)(2,1)}, bf16[3,768,256]{2,1,0:T(8,128)(2,1)}, u32[]{:S(2)}, u32[]{:S(2)}) collective-permute-start(bf16[3,768,256]{2,1,0:T(8,128)(2,1)} %get-tuple-element.218.refs_13_), channel_id=1, source_target_pairs={{0,3},{1,2},{2,1},{3,0},{4,7},{5,6},{6,5},{7,4},{8,11},{9,10},{10,... | collective-permute-start | bytes 3538952 | tf_op jit(solution)/shard_map/ppermute | solution.py:459
  244.0 102.2 %collective-permute-start.4 = (bf16[3,768,256]{2,1,0:T(8,128)(2,1)}, bf16[3,768,256]{2,1,0:T(8,128)(2,1)}, u32[]{:S(2)}, u32[]{:S(2)}) collective-permute-start(bf16[3,768,256]{2,1,0:T(8,128)(2,1)} %get-tuple-element.203.refs_28_), channel_id=1, source_target_pairs={{0,3},{1,2},{2,1},{3,0},{4,7},{5,6},{6,5},{7,4},{8,11},{9,10},{10,... | collective-permute-start | bytes 3538952 | tf_op jit(solution)/shard_map/ppermute | solution.py:459
  299.9 86.4 %collective-permute-start.5 = (bf16[3,768,256]{2,1,0:T(8,128)(2,1)}, bf16[3,768,256]{2,1,0:T(8,128)(2,1)}, u32[]{:S(2)}, u32[]{:S(2)}) collective-permute-start(bf16[3,768,256]{2,1,0:T(8,128)(2,1)} %get-tuple-element.216), channel_id=1, source_target_pairs={{0,3},{1,2},{2,1},{3,0},{4,7},{5,6},{6,5},{7,4},{8,11},{9,10},{10,... | collective-permute-start | bytes 3538952 | tf_op jit(solution)/shard_map/ppermute | solution.py:459
  306.2 80.3 %collective-permute-start.18 = (bf16[3,768,256]{2,1,0:T(8,128)(2,1)}, bf16[3,768,256]{2,1,0:T(8,128)(2,1)}, u32[]{:S(2)}, u32[]{:S(2)}) collective-permute-start(bf16[3,768,256]{2,1,0:T(8,128)(2,1)} %add_convert_fusion.6.refs_14_.refs_15_), channel_id=1, source_target_pairs={{0,1},{1,0},{2,3},{3,2},{4,5},{5,4},{6,7},{7,6},{8,9},{9,8},{10,11... | collective-permute-start | bytes 3538952 | tf_op jit(solution)/shard_map/ppermute | solution.py:459
  344.2 87.7 %collective-permute-start.17 = (bf16[3,768,256]{2,1,0:T(8,128)(2,1)}, bf16[3,768,256]{2,1,0:T(8,128)(2,1)}, u32[]{:S(2)}, u32[]{:S(2)}) collective-permute-start(bf16[3,768,256]{2,1,0:T(8,128)(2,1)} %add_convert_fusion.7.refs_12_.refs_13_), channel_id=1, source_target_pairs={{0,1},{1,0},{2,3},{3,2},{4,5},{5,4},{6,7},{7,6},{8,9},{9,8},{10,11... | collective-permute-start | bytes 3538952 | tf_op jit(solution)/shard_map/ppermute | solution.py:459
  346.2 86.6 %collective-permute-start.11 = (bf16[3,768,256]{2,1,0:T(8,128)(2,1)}, bf16[3,768,256]{2,1,0:T(8,128)(2,1)}, u32[]{:S(2)}, u32[]{:S(2)}) collective-permute-start(bf16[3,768,256]{2,1,0:T(8,128)(2,1)} %get-tuple-element.244.refs_34_), channel_id=1, source_target_pairs={{0,3},{1,2},{2,1},{3,0},{4,7},{5,6},{6,5},{7,4},{8,11},{9,10},{10,... | collective-permute-start | bytes 3538952 | tf_op jit(solution)/shard_map/ppermute | solution.py:459
  386.4 52.9 %collective-permute-start.19 = (bf16[3,768,256]{2,1,0:T(8,128)(2,1)}, bf16[3,768,256]{2,1,0:T(8,128)(2,1)}, u32[]{:S(2)}, u32[]{:S(2)}) collective-permute-start(bf16[3,768,256]{2,1,0:T(8,128)(2,1)} %add_convert_fusion.9.refs_1_.refs_2_), channel_id=1, source_target_pairs={{0,1},{1,0},{2,3},{3,2},{4,5},{5,4},{6,7},{7,6},{8,9},{9,8},{10,11... | collective-permute-start | bytes 3538952 | tf_op jit(solution)/shard_map/ppermute | solution.py:459
  386.5 53.4 %collective-permute-start.16 = (bf16[3,768,256]{2,1,0:T(8,128)(2,1)}, bf16[3,768,256]{2,1,0:T(8,128)(2,1)}, u32[]{:S(2)}, u32[]{:S(2)}) collective-permute-start(bf16[3,768,256]{2,1,0:T(8,128)(2,1)} %get-tuple-element.263), channel_id=1, source_target_pairs={{0,3},{1,2},{2,1},{3,0},{4,7},{5,6},{6,5},{7,4},{8,11},{9,10},{10,... | collective-permute-start | bytes 3538952 | tf_op jit(solution)/shard_map/ppermute | solution.py:459
  387.2 60.3 %collective-permute-start.15 = (bf16[3,768,256]{2,1,0:T(8,128)(2,1)}, bf16[3,768,256]{2,1,0:T(8,128)(2,1)}, u32[]{:S(2)}, u32[]{:S(2)}) collective-permute-start(bf16[3,768,256]{2,1,0:T(8,128)(2,1)} %get-tuple-element.250.refs_23_), channel_id=1, source_target_pairs={{0,3},{1,2},{2,1},{3,0},{4,7},{5,6},{6,5},{7,4},{8,11},{9,10},{10,... | collective-permute-start | bytes 3538952 | tf_op jit(solution)/shard_map/ppermute | solution.py:459
  432.7 62.8 %collective-permute-start.22 = (bf16[3,768,256]{2,1,0:T(8,128)(2,1)}, bf16[3,768,256]{2,1,0:T(8,128)(2,1)}, u32[]{:S(2)}, u32[]{:S(2)}) collective-permute-start(bf16[3,768,256]{2,1,0:T(8,128)(2,1)} %get-tuple-element.287.refs_27_), channel_id=1, source_target_pairs={{0,3},{1,2},{2,1},{3,0},{4,7},{5,6},{6,5},{7,4},{8,11},{9,10},{10,... | collective-permute-start | bytes 3538952 | tf_op jit(solution)/shard_map/ppermute | solution.py:459
  439.3 60.6 %collective-permute-start.14 = (bf16[3,768,256]{2,1,0:T(8,128)(2,1)}, bf16[3,768,256]{2,1,0:T(8,128)(2,1)}, u32[]{:S(2)}, u32[]{:S(2)}) collective-permute-start(bf16[3,768,256]{2,1,0:T(8,128)(2,1)} %add_convert_fusion.4.refs_3_.refs_4_), channel_id=1, source_target_pairs={{0,1},{1,0},{2,3},{3,2},{4,5},{5,4},{6,7},{7,6},{8,9},{9,8},{10,11... | collective-permute-start | bytes 3538952 | tf_op jit(solution)/shard_map/ppermute | solution.py:459
  439.9 71.8 %collective-permute-start.12 = (bf16[3,768,256]{2,1,0:T(8,128)(2,1)}, bf16[3,768,256]{2,1,0:T(8,128)(2,1)}, u32[]{:S(2)}, u32[]{:S(2)}) collective-permute-start(bf16[3,768,256]{2,1,0:T(8,128)(2,1)} %add_convert_fusion.5.refs_1_.refs_2_), channel_id=1, source_target_pairs={{0,1},{1,0},{2,3},{3,2},{4,5},{5,4},{6,7},{7,6},{8,9},{9,8},{10,11... | collective-permute-start | bytes 3538952 | tf_op jit(solution)/shard_map/ppermute | solution.py:459
  447.5 75.2 %collective-permute-start.10 = (bf16[3,768,256]{2,1,0:T(8,128)(2,1)}, bf16[3,768,256]{2,1,0:T(8,128)(2,1)}, u32[]{:S(2)}, u32[]{:S(2)}) collective-permute-start(bf16[3,768,256]{2,1,0:T(8,128)(2,1)} %get-tuple-element.285), channel_id=1, source_target_pairs={{0,3},{1,2},{2,1},{3,0},{4,7},{5,6},{6,5},{7,4},{8,11},{9,10},{10,... | collective-permute-start | bytes 3538952 | tf_op jit(solution)/shard_map/ppermute | solution.py:459
  474.0 63.0 %collective-permute-start.25 = (bf16[3,768,256]{2,1,0:T(8,128)(2,1)}, bf16[3,768,256]{2,1,0:T(8,128)(2,1)}, u32[]{:S(2)}, u32[]{:S(2)}) collective-permute-start(bf16[3,768,256]{2,1,0:T(8,128)(2,1)} %add_convert_fusion.2.refs_3_.refs_4_), channel_id=1, source_target_pairs={{0,1},{1,0},{2,3},{3,2},{4,5},{5,4},{6,7},{7,6},{8,9},{9,8},{10,11... | collective-permute-start | bytes 3538952 | tf_op jit(solution)/shard_map/ppermute | solution.py:459
  495.5 66.8 %collective-permute-start.24 = (bf16[3,768,256]{2,1,0:T(8,128)(2,1)}, bf16[3,768,256]{2,1,0:T(8,128)(2,1)}, u32[]{:S(2)}, u32[]{:S(2)}) collective-permute-start(bf16[3,768,256]{2,1,0:T(8,128)(2,1)} %add_convert_fusion.3.refs_1_.refs_2_), channel_id=1, source_target_pairs={{0,1},{1,0},{2,3},{3,2},{4,5},{5,4},{6,7},{7,6},{8,9},{9,8},{10,11... | collective-permute-start | bytes 3538952 | tf_op jit(solution)/shard_map/ppermute | solution.py:459
  499.8 87.8 %collective-permute-start.23 = (bf16[3,768,256]{2,1,0:T(8,128)(2,1)}, bf16[3,768,256]{2,1,0:T(8,128)(2,1)}, u32[]{:S(2)}, u32[]{:S(2)}) collective-permute-start(bf16[3,768,256]{2,1,0:T(8,128)(2,1)} %add_convert_fusion.refs_1_.refs_2_), channel_id=1, source_target_pairs={{0,1},{1,0},{2,3},{3,2},{4,5},{5,4},{6,7},{7,6},{8,9},{9,8},{10,11... | collective-permute-start | bytes 3538952 | tf_op jit(solution)/shard_map/ppermute | solution.py:459
  525.6 80.0 %collective-permute-start.21 = (bf16[3,768,256]{2,1,0:T(8,128)(2,1)}, bf16[3,768,256]{2,1,0:T(8,128)(2,1)}, u32[]{:S(2)}, u32[]{:S(2)}) collective-permute-start(bf16[3,768,256]{2,1,0:T(8,128)(2,1)} %add_convert_fusion.1.refs_3_.refs_4_), channel_id=1, source_target_pairs={{0,1},{1,0},{2,3},{3,2},{4,5},{5,4},{6,7},{7,6},{8,9},{9,8},{10,11... | collective-permute-start | bytes 3538952 | tf_op jit(solution)/shard_map/ppermute | solution.py:459
  (4 other events, 95.0 us)

commit v3 on v2

--- a/solution.py
+++ b/solution.py
@@ -420,7 +420,7 @@
 
 
 def adamw_jobs(half, jobs, arrays, so_far, after):
-    steps = 4 * len(jobs)
+    steps = 2 * len(jobs)
     beside = Beside(jobs, arrays, so_far, steps)
     return call(
         functools.partial(adamw_jobs_kernel, beside),
@@ -504,15 +504,13 @@
             saved = [[], []]
             start = 0
             while start < pieces:
-                group = 1 if is_last and start < GROUP else GROUP
+                group = GROUP
                 sides = [(*kept[s][layer][1:], *by_h[s]) for s in range(2)]
                 if is_last:
                     sides[0] = (kept[0][layer][2], *own_last)
                 jobs = []
                 if not is_last and start == 0 and len(other_steps) >= 2 * GROUP:
                     jobs.append(job(False, other_steps))
-                elif not is_last and start == GROUP and len(own_steps) >= GROUP:
-                    jobs.append(job(True, own_steps))
                 made = run(weight_gradient, mine, sides, weights, layer, start, group, keep, jobs, arrays, state["new"])
                 sums += [(layer, start + k, part, send(part, pair_b)) for k, part in enumerate(made[:group])]
                 if jobs:
@@ -524,7 +522,13 @@
                             by_h[s] = (by_h[s][0], made.pop(0))
                         if keep:
                             saved[s] += [made.pop(0), made.pop(0)]
-                while len(sums) > (3 if is_last or start else 2):
+                left = 2 if not is_last and start == 0 else 3
+                if is_last and start + group >= pieces:
+                    while len(sums) > left + 1:
+                        merge_next()
+                    if len(own_steps) >= GROUP:
+                        state["new"] = run(adamw_jobs, mine, [job(True, own_steps)], arrays, state["new"])[1:]
+                while len(sums) > left:
                     merge_next()
                 if not is_last and start == GROUP:
                     if len(own_steps) >= GROUP:

time: 619 us -> 604 us (0.976)
  waiting for transfers between devices: 69.9 us -> 59.4 us
  Pallas kernels: 474 us -> 466 us
    ppermute x26, waiting for transfers between devices: 69.9 us -> 59.4 us  [send(): return lax.ppermute(array, 'dp', pairs)]
    pallas_call x18, Pallas kernels: 474 us -> 466 us  [call(): pl.pallas_call(body, grid_spec=pltpu.PrefetchScalarGridSpec(num_scalar_pr...]
  transfers between devices with their start and end apart: 26 -> 26, of which waited for: 7 -> 6; matrix products, arithmetic and copies ran while one was open for 6% -> 6% of each run, Pallas kernels for 71% -> 73%
where the time goes in v3:
time: 604 us; the launch traced here: 598 us
  Pallas kernels  466 us (77%)
  waiting for transfers between devices  59.4 us (10%)
  starting transfers between devices  37.7 us (6%)
  other arithmetic  33.8 us (6%)
    pallas_call x18, Pallas kernels, call(): pl.pallas_call(body, grid_spec=pltpu.PrefetchScalarGridSpec(num_scalar_pr...  466 us
    ppermute x26, waiting for transfers between devices, send(): return lax.ppermute(array, 'dp', pairs)  59.4 us
    ppermute x26, starting transfers between devices, send(): return lax.ppermute(array, 'dp', pairs)  37.7 us
    convert_element_type x12, other arithmetic, merge_next(): whole = (part.astype(F32) + came.astype(F32)).astype(BF16)  33.8 us
  transfers between devices with their start and end apart: 26, of which 6 were waited for; matrix products, arithmetic and copies ran while one was open for 6% of the time, Pallas kernels for 73%

profile of v3, /device:TPU:112, one launch (start us, length us, event | category | flops | bytes accessed | tf_op | source)
XLA Modules:
  0.0 598.3 jit_solution(17417036868123006957)
XLA Ops:
  3.2 39.8 %shard_map.178 = (bf16[2048,768]{1,0:T(8,128)(2,1)}, bf16[768,2048]{1,0:T(8,128)(2,1)}, bf16[2048,768]{1,0:T(8,128)(2,1)}, bf16[2048,768]{1,0:T(8,128)(2,1)}, bf16[768,2048]{1,0:T(8,128)(2,1)}) custom-call(bf16[2048,768]{1,0:T(8,128)(2,1)} %bitcast.4, bf16[2,768,3072]{2,1,0:T(8,128)(2,1)} %refs_2_.7, bf16[2,768,3072]{2,1,0:T(8,128)(2,1)} %refs_3_.7, ...), custom_call_target="tpu_custom_call" | custom-call | flops 1 | tf_op jit(solution)/shard_map/pallas_call | solution.py:39
  42.9 64.2 %shard_map.179 = (bf16[2048,768]{1,0:T(8,128)(2,1)}, bf16[768,2048]{1,0:T(8,128)(2,1)}, bf16[768,2048]{1,0:T(8,128)(2,1)}, bf16[2048,1536]{1,0:T(8,128)(2,1)}, b...) custom-call(s32[1]{0:T(128)} %bitcast.refs_0_, bf16[2048,768]{1,0:T(8,128)(2,1)} %get-tuple-element.160.refs_1_, ...), custom_call_target="tpu_custom_call" | custom-call | flops 1 | tf_op jit(solution)/shard_map/pallas_call | solution.py:39
  107.2 40.0 %shard_map.180 = (bf16[2048,768]{1,0:T(8,128)(2,1)}, bf16[768,2048]{1,0:T(8,128)(2,1)}, bf16[2048,768]{1,0:T(8,128)(2,1)}, bf16[2048,768]{1,0:T(8,128)(2,1)}, bf16[768,2048]{1,0:T(8,128)(2,1)}) custom-call(bf16[2048,768]{1,0:T(8,128)(2,1)} %collective-permute-done.refs_0_, bf16[2,768,3072]{2,1,0:T(8,128)(2,1)} %refs_2_.7, bf16[2,768,3072]{2,1,0:T(8,128)(2,1)} %refs_3_.7, ...), custom_call_target="tpu_custom_call" | custom-call | flops 1 | tf_op jit(solution)/shard_map/pallas_call | solution.py:39
  147.2 22.8 %shard_map.181 = (bf16[3,768,256]{2,1,0:T(8,128)(2,1)}, bf16[3,768,256]{2,1,0:T(8,128)(2,1)}, bf16[768,2048]{1,0:T(8,128)(2,1)}, bf16[2048,512]{1,0:T(8,128)(2,1)}, bf16[2048,512]{1,0:T(8,128)(2,1)}) custom-call(s32[1]{0:T(128)} %bitcast.refs_0_, bf16[768,2048]{1,0:T(8,128)(2,1)} %get-tuple-element.168.refs_1_, ...), custom_call_target="tpu_custom_call" | custom-call | flops 1 | tf_op jit(solution)/shard_map/pallas_call | solution.py:39
  170.0 3.5 collective-permute-start.3
  173.6 23.1 %shard_map.182 = (bf16[3,768,256]{2,1,0:T(8,128)(2,1)}, bf16[3,768,256]{2,1,0:T(8,128)(2,1)}, bf16[2048,512]{1,0:T(8,128)(2,1)}, bf16[2048,512]{1,0:T(8,128)(2,1)}) custom-call(s32[1]{0:T(128)} %bitcast.refs_0_, bf16[768,2048]{1,0:T(8,128)(2,1)} %get-tuple-element.168.refs_1_, bf16[768,2048]{1,0:T(8,128)(2,1)} %get-tuple-element.169.refs_2_, ...), custom_call_target="tpu_custom_call" | custom-call | flops 1 | tf_op jit(solution)/shard_map/pallas_call | solution.py:39
  200.1 22.8 %shard_map.183 = (bf16[3,768,256]{2,1,0:T(8,128)(2,1)}, bf16[3,768,256]{2,1,0:T(8,128)(2,1)}, bf16[2048,512]{1,0:T(8,128)(2,1)}, bf16[2048,512]{1,0:T(8,128)(2,1)}) custom-call(s32[1]{0:T(128)} %bitcast.refs_0_, bf16[768,2048]{1,0:T(8,128)(2,1)} %get-tuple-element.168.refs_1_, bf16[768,2048]{1,0:T(8,128)(2,1)} %get-tuple-element.169.refs_2_, ...), custom_call_target="tpu_custom_call" | custom-call | flops 1 | tf_op jit(solution)/shard_map/pallas_call | solution.py:39
  236.8 10.4 %shard_map.184 = (f32[8,128]{1,0:T(8,128)}, bf16[2,768,3072]{2,1,0:T(8,128)(2,1)}, bf16[2,768,3072]{2,1,0:T(8,128)(2,1)}, bf16[2,3072,768]{2,1,0:T(8,128)(2,1)},...) custom-call(s32[1]{0:T(128)} %bitcast.refs_0_, ...), custom_call_target="tpu_custom_call" | custom-call | flops 1 | tf_op jit(solution)/shard_map/pallas_call | solution.py:39
  247.2 48.1 %shard_map.185 = (bf16[2048,768]{1,0:T(8,128)(2,1)}, bf16[768,2048]{1,0:T(8,128)(2,1)}) custom-call(s32[1]{0:T(128)} %bitcast.refs_0_, bf16[2048,768]{1,0:T(8,128)(2,1)} %get-tuple-element.166.refs_1_, bf16[2048,768]{1,0:T(8,128)(2,1)} %get-tuple-element.167.refs_6_.refs_2_, bf16[2048,768]{1,0:T(8,128)(2,1)} %collective-permute-done.1.refs_8_.refs_3_, ...), custom_call_target="tpu_custom_call" | custom-call | flops 1 | tf_op jit(solution)/shard_map/pallas_call | solution.py:39
  303.1 34.7 %shard_map.186 = (bf16[3,768,256]{2,1,0:T(8,128)(2,1)}, bf16[3,768,256]{2,1,0:T(8,128)(2,1)}, bf16[2,768,3072]{2,1,0:T(8,128)(2,1)}, bf16[2,768,3072]{2,1,0:T(8,...) custom-call(s32[1]{0:T(128)} %bitcast.refs_0_, ...), custom_call_target="tpu_custom_call", output_to_operand_aliasing={{2}: (25, {}), {3}: (26, {}), {4}: (27, {}), {5}: (28, {}),... | custom-call | flops 1 | tf_op jit(solution)/shard_map/pallas_call | solution.py:39
  344.1 28.1 %shard_map.187 = (bf16[3,768,256]{2,1,0:T(8,128)(2,1)}, bf16[3,768,256]{2,1,0:T(8,128)(2,1)}) custom-call(s32[1]{0:T(128)} %bitcast.refs_0_, bf16[2048,768]{1,0:T(8,128)(2,1)} %get-tuple-element.158.refs_7_.refs_1_, bf16[768,2048]{1,0:T(8,128)(2,1)} %get-tuple-element.159.refs_2_, bf16[2048,768]{1,0:T(8,128)(2,1)} %get-tuple-element.162.refs_4_.refs_3_, ...), custom_call_target="tpu_custom_call" | custom-call | flops 1 | tf_op jit(solution)/shard_map/pallas_call | solution.py:39
  377.2 10.8 %shard_map.188 = (f32[8,128]{1,0:T(8,128)}, bf16[2,768,3072]{2,1,0:T(8,128)(2,1)}, bf16[2,768,3072]{2,1,0:T(8,128)(2,1)}, bf16[2,3072,768]{2,1,0:T(8,128)(2,1)},...) custom-call(s32[1]{0:T(128)} %bitcast.refs_0_, ...), custom_call_target="tpu_custom_call", output_to_operand_aliasing={{1}: (14, {}), {2}: (15, {}), {3}: (16, {}), {4}: (17, {}),... | custom-call | flops 1 | tf_op jit(solution)/shard_map/pallas_call | solution.py:39
  388.0 28.1 %shard_map.189 = (bf16[3,768,256]{2,1,0:T(8,128)(2,1)}, bf16[3,768,256]{2,1,0:T(8,128)(2,1)}) custom-call(s32[1]{0:T(128)} %bitcast.refs_0_, bf16[2048,768]{1,0:T(8,128)(2,1)} %get-tuple-element.158.refs_7_.refs_1_, bf16[768,2048]{1,0:T(8,128)(2,1)} %get-tuple-element.159.refs_2_, bf16[2048,768]{1,0:T(8,128)(2,1)} %get-tuple-element.162.refs_4_.refs_3_, ...), custom_call_target="tpu_custom_call" | custom-call | flops 1 | tf_op jit(solution)/shard_map/pallas_call | solution.py:39
  430.1 16.4 %collective-permute-done.22 = bf16[3,768,256]{2,1,0:T(8,128)(2,1)} collective-permute-done((bf16[3,768,256]{2,1,0:T(8,128)(2,1)}, bf16[3,768,256]{2,1,0:T(8,128)(2,1)}, u32[]{:S(2)}, u32[]{:S(2)}) %collective-permute-start.22) | collective-permute-done | bytes 1179680 | tf_op jit(solution)/shard_map/ppermute | solution.py:459
  449.7 19.8 %shard_map.190 = (f32[8,128]{1,0:T(8,128)}, bf16[2,768,3072]{2,1,0:T(8,128)(2,1)}, bf16[2,768,3072]{2,1,0:T(8,128)(2,1)}, bf16[2,3072,768]{2,1,0:T(8,128)(2,1)},...) custom-call(s32[1]{0:T(128)} %bitcast.refs_0_, ...), custom_call_target="tpu_custom_call", output_to_operand_aliasing={{1}: (18, {}), {2}: (19, {}), {3}: (20, {}), {4}: (21, {}),... | custom-call | flops 1 | tf_op jit(solution)/shard_map/pallas_call | solution.py:39
  469.5 20.1 %shard_map.191 = (f32[8,128]{1,0:T(8,128)}, bf16[2,768,3072]{2,1,0:T(8,128)(2,1)}, bf16[2,768,3072]{2,1,0:T(8,128)(2,1)}, bf16[2,3072,768]{2,1,0:T(8,128)(2,1)},...) custom-call(s32[1]{0:T(128)} %bitcast.refs_0_, ...), custom_call_target="tpu_custom_call", output_to_operand_aliasing={{1}: (18, {}), {2}: (19, {}), {3}: (20, {}), {4}: (21, {}),... | custom-call | flops 1 | tf_op jit(solution)/shard_map/pallas_call | solution.py:39
  489.6 7.5 %collective-permute-done.9 = bf16[3,768,256]{2,1,0:T(8,128)(2,1)} collective-permute-done((bf16[3,768,256]{2,1,0:T(8,128)(2,1)}, bf16[3,768,256]{2,1,0:T(8,128)(2,1)}, u32[]{:S(2)}, u32[]{:S(2)}) %collective-permute-start.9) | collective-permute-done | bytes 1179680 | tf_op jit(solution)/shard_map/ppermute | solution.py:459
  507.4 19.8 %shard_map.192 = (f32[8,128]{1,0:T(8,128)}, bf16[2,768,3072]{2,1,0:T(8,128)(2,1)}, bf16[2,768,3072]{2,1,0:T(8,128)(2,1)}, bf16[2,3072,768]{2,1,0:T(8,128)(2,1)},...) custom-call(s32[1]{0:T(128)} %bitcast.refs_0_, ...), custom_call_target="tpu_custom_call", output_to_operand_aliasing={{1}: (18, {}), {2}: (19, {}), {3}: (20, {}), {4}: (21, {}),... | custom-call | flops 1 | tf_op jit(solution)/shard_map/pallas_call | solution.py:39
  532.2 22.3 %collective-permute-done.24.refs_5_.refs_6_ = bf16[3,768,256]{2,1,0:T(8,128)(2,1)} collective-permute-done((bf16[3,768,256]{2,1,0:T(8,128)(2,1)}, bf16[3,768,256]{2,1,0:T(8,128)(2,1)}, u32[]{:S(2)}, u32[]{:S(2)}) %collective-permute-start.24) | collective-permute-done | bytes 1179680 | tf_op jit(solution)/shard_map/ppermute | solution.py:459
  554.5 20.0 %shard_map.193 = (f32[8,128]{1,0:T(8,128)}, bf16[2,768,3072]{2,1,0:T(8,128)(2,1)}, bf16[2,768,3072]{2,1,0:T(8,128)(2,1)}, bf16[2,3072,768]{2,1,0:T(8,128)(2,1)},...) custom-call(s32[1]{0:T(128)} %bitcast.refs_0_, ...), custom_call_target="tpu_custom_call", output_to_operand_aliasing={{1}: (18, {}), {2}: (19, {}), {3}: (20, {}), {4}: (21, {}),... | custom-call | flops 1 | tf_op jit(solution)/shard_map/pallas_call | solution.py:39
  574.5 4.2 collective-permute-done.23.refs_1_
  578.7 6.7 %shard_map.194 = (f32[8,128]{1,0:T(8,128)}, bf16[2,768,3072]{2,1,0:T(8,128)(2,1)}, bf16[2,768,3072]{2,1,0:T(8,128)(2,1)}, bf16[2,3072,768]{2,1,0:T(8,128)(2,1)},...) custom-call(s32[1]{0:T(128)S(6)} %sub.8.refs_0_, ...), custom_call_target="tpu_custom_call", output_to_operand_aliasing={{1}: (11, {}), {2}: (12, {}), {3}: (13, {}), {4}: (14, {}),... | custom-call | flops 1 | tf_op jit(solution)/shard_map/pallas_call | solution.py:39
  585.4 5.9 collective-permute-done.21.refs_1_
  591.3 6.7 %shard_map.195 = (f32[8,128]{1,0:T(8,128)}, bf16[2,768,3072]{2,1,0:T(8,128)(2,1)}, bf16[2,768,3072]{2,1,0:T(8,128)(2,1)}, bf16[2,3072,768]{2,1,0:T(8,128)(2,1)},...) custom-call(s32[1]{0:T(128)S(6)} %sub.8.refs_0_, ...), custom_call_target="tpu_custom_call", output_to_operand_aliasing={{1}: (11, {}), {2}: (12, {}), {3}: (13, {}), {4}: (14, {}),... | custom-call | flops 1 | tf_op jit(solution)/shard_map/pallas_call | solution.py:39
  (68 shorter events, 71.2 us)
Async XLA Ops:
  0.6 106.5 %collective-permute-start = (bf16[2048,768]{1,0:T(8,128)(2,1)}, bf16[2048,768]{1,0:T(8,128)(2,1)}, u32[]{:S(2)}, u32[]{:S(2)}) collective-permute-start(bf16[2048,768]{1,0:T(8,128)(2,1)} %bitcast.3), channel_id=1, source_target_pairs={{0,1},{1,0},{2,3},{3,2},{4,5},{5,4},{6,7},{7,6},{8,9},{9,8},{10,11... | collective-permute-start | bytes 9437192 | tf_op jit(solution)/shard_map/ppermute | solution.py:459
  3.1 144.2 %collective-permute-start.1 = (bf16[2048,768]{1,0:T(8,128)(2,1)}, bf16[2048,768]{1,0:T(8,128)(2,1)}, u32[]{:S(2)}, u32[]{:S(2)}) collective-permute-start(bf16[2048,768]{1,0:T(8,128)(2,1)} %bitcast.5), channel_id=1, source_target_pairs={{0,1},{1,0},{2,3},{3,2},{4,5},{5,4},{6,7},{7,6},{8,9},{9,8},{10,11... | collective-permute-start | bytes 9437192 | tf_op jit(solution)/shard_map/ppermute | solution.py:459
  170.0 52.9 %collective-permute-start.3 = (bf16[3,768,256]{2,1,0:T(8,128)(2,1)}, bf16[3,768,256]{2,1,0:T(8,128)(2,1)}, u32[]{:S(2)}, u32[]{:S(2)}) collective-permute-start(bf16[3,768,256]{2,1,0:T(8,128)(2,1)} %get-tuple-element.187), channel_id=1, source_target_pairs={{0,3},{1,2},{2,1},{3,0},{4,7},{5,6},{6,5},{7,4},{8,11},{9,10},{10,... | collective-permute-start | bytes 3538952 | tf_op jit(solution)/shard_map/ppermute | solution.py:459
  173.5 52.4 %collective-permute-start.2 = (bf16[3,768,256]{2,1,0:T(8,128)(2,1)}, bf16[3,768,256]{2,1,0:T(8,128)(2,1)}, u32[]{:S(2)}, u32[]{:S(2)}) collective-permute-start(bf16[3,768,256]{2,1,0:T(8,128)(2,1)} %get-tuple-element.183.refs_13_), channel_id=1, source_target_pairs={{0,3},{1,2},{2,1},{3,0},{4,7},{5,6},{6,5},{7,4},{8,11},{9,10},{10,... | collective-permute-start | bytes 3538952 | tf_op jit(solution)/shard_map/ppermute | solution.py:459
  196.8 98.5 %collective-permute-start.5 = (bf16[3,768,256]{2,1,0:T(8,128)(2,1)}, bf16[3,768,256]{2,1,0:T(8,128)(2,1)}, u32[]{:S(2)}, u32[]{:S(2)}) collective-permute-start(bf16[3,768,256]{2,1,0:T(8,128)(2,1)} %get-tuple-element.195), channel_id=1, source_target_pairs={{0,3},{1,2},{2,1},{3,0},{4,7},{5,6},{6,5},{7,4},{8,11},{9,10},{10,... | collective-permute-start | bytes 3538952 | tf_op jit(solution)/shard_map/ppermute | solution.py:459
  200.0 98.4 %collective-permute-start.4 = (bf16[3,768,256]{2,1,0:T(8,128)(2,1)}, bf16[3,768,256]{2,1,0:T(8,128)(2,1)}, u32[]{:S(2)}, u32[]{:S(2)}) collective-permute-start(bf16[3,768,256]{2,1,0:T(8,128)(2,1)} %get-tuple-element.192.refs_13_), channel_id=1, source_target_pairs={{0,3},{1,2},{2,1},{3,0},{4,7},{5,6},{6,5},{7,4},{8,11},{9,10},{10,... | collective-permute-start | bytes 3538952 | tf_op jit(solution)/shard_map/ppermute | solution.py:459
  228.9 72.2 %collective-permute-start.7 = (bf16[3,768,256]{2,1,0:T(8,128)(2,1)}, bf16[3,768,256]{2,1,0:T(8,128)(2,1)}, u32[]{:S(2)}, u32[]{:S(2)}) collective-permute-start(bf16[3,768,256]{2,1,0:T(8,128)(2,1)} %add_convert_fusion.10.refs_3_.refs_4_), channel_id=1, source_target_pairs={{0,1},{1,0},{2,3},{3,2},{4,5},{5,4},{6,7},{7,6},{8,9},{9,8},{10,11... | collective-permute-start | bytes 3538952 | tf_op jit(solution)/shard_map/ppermute | solution.py:459
  232.0 71.1 %collective-permute-start.6 = (bf16[3,768,256]{2,1,0:T(8,128)(2,1)}, bf16[3,768,256]{2,1,0:T(8,128)(2,1)}, u32[]{:S(2)}, u32[]{:S(2)}) collective-permute-start(bf16[3,768,256]{2,1,0:T(8,128)(2,1)} %add_convert_fusion.11.refs_1_.refs_2_), channel_id=1, source_target_pairs={{0,1},{1,0},{2,3},{3,2},{4,5},{5,4},{6,7},{7,6},{8,9},{9,8},{10,11... | collective-permute-start | bytes 3538952 | tf_op jit(solution)/shard_map/ppermute | solution.py:459
  233.6 107.4 %collective-permute-start.11 = (bf16[3,768,256]{2,1,0:T(8,128)(2,1)}, bf16[3,768,256]{2,1,0:T(8,128)(2,1)}, u32[]{:S(2)}, u32[]{:S(2)}) collective-permute-start(bf16[3,768,256]{2,1,0:T(8,128)(2,1)} %get-tuple-element.223.refs_14_), channel_id=1, source_target_pairs={{0,3},{1,2},{2,1},{3,0},{4,7},{5,6},{6,5},{7,4},{8,11},{9,10},{10,... | collective-permute-start | bytes 3538952 | tf_op jit(solution)/shard_map/ppermute | solution.py:459
  295.3 76.9 %collective-permute-start.12 = (bf16[3,768,256]{2,1,0:T(8,128)(2,1)}, bf16[3,768,256]{2,1,0:T(8,128)(2,1)}, u32[]{:S(2)}, u32[]{:S(2)}) collective-permute-start(bf16[3,768,256]{2,1,0:T(8,128)(2,1)} %get-tuple-element.226), channel_id=1, source_target_pairs={{0,3},{1,2},{2,1},{3,0},{4,7},{5,6},{6,5},{7,4},{8,11},{9,10},{10,... | collective-permute-start | bytes 3538952 | tf_op jit(solution)/shard_map/ppermute | solution.py:459
  298.4 76.8 %collective-permute-start.14 = (bf16[3,768,256]{2,1,0:T(8,128)(2,1)}, bf16[3,768,256]{2,1,0:T(8,128)(2,1)}, u32[]{:S(2)}, u32[]{:S(2)}) collective-permute-start(bf16[3,768,256]{2,1,0:T(8,128)(2,1)} %add_convert_fusion.8.refs_3_.refs_4_), channel_id=1, source_target_pairs={{0,1},{1,0},{2,3},{3,2},{4,5},{5,4},{6,7},{7,6},{8,9},{9,8},{10,11... | collective-permute-start | bytes 3538952 | tf_op jit(solution)/shard_map/ppermute | solution.py:459
  301.1 115.1 %collective-permute-start.13 = (bf16[3,768,256]{2,1,0:T(8,128)(2,1)}, bf16[3,768,256]{2,1,0:T(8,128)(2,1)}, u32[]{:S(2)}, u32[]{:S(2)}) collective-permute-start(bf16[3,768,256]{2,1,0:T(8,128)(2,1)} %add_convert_fusion.9.refs_1_.refs_2_), channel_id=1, source_target_pairs={{0,1},{1,0},{2,3},{3,2},{4,5},{5,4},{6,7},{7,6},{8,9},{9,8},{10,11... | collective-permute-start | bytes 3538952 | tf_op jit(solution)/shard_map/ppermute | solution.py:459
  337.8 81.5 %collective-permute-start.17 = (bf16[3,768,256]{2,1,0:T(8,128)(2,1)}, bf16[3,768,256]{2,1,0:T(8,128)(2,1)}, u32[]{:S(2)}, u32[]{:S(2)}) collective-permute-start(bf16[3,768,256]{2,1,0:T(8,128)(2,1)} %get-tuple-element.243), channel_id=1, source_target_pairs={{0,3},{1,2},{2,1},{3,0},{4,7},{5,6},{6,5},{7,4},{8,11},{9,10},{10,... | collective-permute-start | bytes 3538952 | tf_op jit(solution)/shard_map/ppermute | solution.py:459
  341.0 78.4 %collective-permute-start.15 = (bf16[3,768,256]{2,1,0:T(8,128)(2,1)}, bf16[3,768,256]{2,1,0:T(8,128)(2,1)}, u32[]{:S(2)}, u32[]{:S(2)}) collective-permute-start(bf16[3,768,256]{2,1,0:T(8,128)(2,1)} %get-tuple-element.240.refs_12_), channel_id=1, source_target_pairs={{0,3},{1,2},{2,1},{3,0},{4,7},{5,6},{6,5},{7,4},{8,11},{9,10},{10,... | collective-permute-start | bytes 3538952 | tf_op jit(solution)/shard_map/ppermute | solution.py:459
  372.2 55.9 %collective-permute-start.19 = (bf16[3,768,256]{2,1,0:T(8,128)(2,1)}, bf16[3,768,256]{2,1,0:T(8,128)(2,1)}, u32[]{:S(2)}, u32[]{:S(2)}) collective-permute-start(bf16[3,768,256]{2,1,0:T(8,128)(2,1)} %add_convert_fusion.6.refs_1_.refs_2_), channel_id=1, source_target_pairs={{0,1},{1,0},{2,3},{3,2},{4,5},{5,4},{6,7},{7,6},{8,9},{9,8},{10,11... | collective-permute-start | bytes 3538952 | tf_op jit(solution)/shard_map/ppermute | solution.py:459
  375.2 52.9 %collective-permute-start.20 = (bf16[3,768,256]{2,1,0:T(8,128)(2,1)}, bf16[3,768,256]{2,1,0:T(8,128)(2,1)}, u32[]{:S(2)}, u32[]{:S(2)}) collective-permute-start(bf16[3,768,256]{2,1,0:T(8,128)(2,1)} %add_convert_fusion.5.refs_3_.refs_4_), channel_id=1, source_target_pairs={{0,1},{1,0},{2,3},{3,2},{4,5},{5,4},{6,7},{7,6},{8,9},{9,8},{10,11... | collective-permute-start | bytes 3538952 | tf_op jit(solution)/shard_map/ppermute | solution.py:459
  419.3 70.3 %collective-permute-start.10 = (bf16[3,768,256]{2,1,0:T(8,128)(2,1)}, bf16[3,768,256]{2,1,0:T(8,128)(2,1)}, u32[]{:S(2)}, u32[]{:S(2)}) collective-permute-start(bf16[3,768,256]{2,1,0:T(8,128)(2,1)} %get-tuple-element.238), channel_id=1, source_target_pairs={{0,3},{1,2},{2,1},{3,0},{4,7},{5,6},{6,5},{7,4},{8,11},{9,10},{10,... | collective-permute-start | bytes 3538952 | tf_op jit(solution)/shard_map/ppermute | solution.py:459
  419.4 77.7 %collective-permute-start.9 = (bf16[3,768,256]{2,1,0:T(8,128)(2,1)}, bf16[3,768,256]{2,1,0:T(8,128)(2,1)}, u32[]{:S(2)}, u32[]{:S(2)}) collective-permute-start(bf16[3,768,256]{2,1,0:T(8,128)(2,1)} %get-tuple-element.220.refs_23_), channel_id=1, source_target_pairs={{0,3},{1,2},{2,1},{3,0},{4,7},{5,6},{6,5},{7,4},{8,11},{9,10},{10,... | collective-permute-start | bytes 3538952 | tf_op jit(solution)/shard_map/ppermute | solution.py:459
  428.1 79.2 %collective-permute-start.18 = (bf16[3,768,256]{2,1,0:T(8,128)(2,1)}, bf16[3,768,256]{2,1,0:T(8,128)(2,1)}, u32[]{:S(2)}, u32[]{:S(2)}) collective-permute-start(bf16[3,768,256]{2,1,0:T(8,128)(2,1)} %add_convert_fusion.2.refs_3_.refs_4_), channel_id=1, source_target_pairs={{0,1},{1,0},{2,3},{3,2},{4,5},{5,4},{6,7},{7,6},{8,9},{9,8},{10,11... | collective-permute-start | bytes 3538952 | tf_op jit(solution)/shard_map/ppermute | solution.py:459
  428.1 79.3 %collective-permute-start.16 = (bf16[3,768,256]{2,1,0:T(8,128)(2,1)}, bf16[3,768,256]{2,1,0:T(8,128)(2,1)}, u32[]{:S(2)}, u32[]{:S(2)}) collective-permute-start(bf16[3,768,256]{2,1,0:T(8,128)(2,1)} %add_convert_fusion.3.refs_1_.refs_2_), channel_id=1, source_target_pairs={{0,1},{1,0},{2,3},{3,2},{4,5},{5,4},{6,7},{7,6},{8,9},{9,8},{10,11... | collective-permute-start | bytes 3538952 | tf_op jit(solution)/shard_map/ppermute | solution.py:459
  446.6 80.7 %collective-permute-start.8 = (bf16[3,768,256]{2,1,0:T(8,128)(2,1)}, bf16[3,768,256]{2,1,0:T(8,128)(2,1)}, u32[]{:S(2)}, u32[]{:S(2)}) collective-permute-start(bf16[3,768,256]{2,1,0:T(8,128)(2,1)} %get-tuple-element.265), channel_id=1, source_target_pairs={{0,3},{1,2},{2,1},{3,0},{4,7},{5,6},{6,5},{7,4},{8,11},{9,10},{10,... | collective-permute-start | bytes 3538952 | tf_op jit(solution)/shard_map/ppermute | solution.py:459
  502.8 51.7 %collective-permute-start.24 = (bf16[3,768,256]{2,1,0:T(8,128)(2,1)}, bf16[3,768,256]{2,1,0:T(8,128)(2,1)}, u32[]{:S(2)}, u32[]{:S(2)}) collective-permute-start(bf16[3,768,256]{2,1,0:T(8,128)(2,1)} %add_convert_fusion.7.refs_1_.refs_2_), channel_id=1, source_target_pairs={{0,1},{1,0},{2,3},{3,2},{4,5},{5,4},{6,7},{7,6},{8,9},{9,8},{10,11... | collective-permute-start | bytes 3538952 | tf_op jit(solution)/shard_map/ppermute | solution.py:459
  507.3 71.3 %collective-permute-start.23 = (bf16[3,768,256]{2,1,0:T(8,128)(2,1)}, bf16[3,768,256]{2,1,0:T(8,128)(2,1)}, u32[]{:S(2)}, u32[]{:S(2)}) collective-permute-start(bf16[3,768,256]{2,1,0:T(8,128)(2,1)} %add_convert_fusion.refs_1_.refs_2_), channel_id=1, source_target_pairs={{0,1},{1,0},{2,3},{3,2},{4,5},{5,4},{6,7},{7,6},{8,9},{9,8},{10,11... | collective-permute-start | bytes 3538952 | tf_op jit(solution)/shard_map/ppermute | solution.py:459
  530.2 61.1 %collective-permute-start.21 = (bf16[3,768,256]{2,1,0:T(8,128)(2,1)}, bf16[3,768,256]{2,1,0:T(8,128)(2,1)}, u32[]{:S(2)}, u32[]{:S(2)}) collective-permute-start(bf16[3,768,256]{2,1,0:T(8,128)(2,1)} %add_convert_fusion.1.refs_3_.refs_4_), channel_id=1, source_target_pairs={{0,1},{1,0},{2,3},{3,2},{4,5},{5,4},{6,7},{7,6},{8,9},{9,8},{10,11... | collective-permute-start | bytes 3538952 | tf_op jit(solution)/shard_map/ppermute | solution.py:459
  (7 other events, 96.7 us)
